TPU v7x, 32 devices: a 4x4x1 block of a 4x4x8 slice. The times are simulated.
32 devices in a mesh: dp: 1 (over z), tp: 4 (over y), sq: 8 (over x, core).
Axes of the slice: x: 4, y: 4, z: 1, core: 2. Of those that a mesh axis runs over, the one named last changes fastest.
The devices are a block of a 4x4x8 slice.
Arguments:
- hidden: bfloat16 [256, 6144], P('dp')
- cache_lens: int32 [256], P('dp')
- k_cache: bfloat16 [256, 2048, 128], P('dp', 'sq')
- v_cache: bfloat16 [256, 2048, 128], P('dp', 'sq')
- ln_gain: float32 [6144], replicated
- ln_bias: float32 [6144], replicated
- w_query: bfloat16 [6144, 6144], P(None, 'tp')
- b_query: float32 [6144], P('tp')
- w_kv: bfloat16 [6144, 256], replicated
- b_kv: float32 [256], replicated
- w_out: bfloat16 [6144, 6144], P('tp')
- b_out: float32 [6144], replicated
Outputs:
- output 1: bfloat16 [256, 6144], P('dp')
- output 2: bfloat16 [256, 2048, 128], P('dp', 'sq')
- output 3: bfloat16 [256, 2048, 128], P('dp', 'sq')
All inputs are finite; a program needn't handle non-finite values.
Results may differ from a plain program's by a relative error of at most 0.00348177.
Values sent between devices are 32-bit elements.
A program may use at most 768 MiB of HBM per device.

v0:
```python
import jax
import jax.numpy as jnp
from jax import lax
from jax.sharding import PartitionSpec as P


def layer_norm(x_rows, ln_gain, ln_bias):
    x_wide = x_rows.astype(jnp.float32)
    mean_val = jnp.mean(x_wide, axis=-1, keepdims=True)
    centered = x_wide - mean_val
    variance = jnp.mean(centered * centered, axis=-1, keepdims=True)
    normed = centered * lax.rsqrt(variance + 1e-5)
    return (normed * ln_gain + ln_bias).astype(jnp.bfloat16)


def solution(mesh):
    def local_step(hidden, cache_lens, k_cache, v_cache, ln_gain, ln_bias, w_query, b_query, w_kv, b_kv, w_out, b_out):
        batch, pos_local, head_dim = k_cache.shape
        heads_local = w_query.shape[1] // head_dim
        normed = layer_norm(hidden, ln_gain, ln_bias)
        query = (jnp.dot(normed, w_query, preferred_element_type=jnp.float32) + b_query).astype(jnp.bfloat16)
        query = query.reshape(batch, heads_local, head_dim)
        key_val = (jnp.dot(normed, w_kv, preferred_element_type=jnp.float32) + b_kv).astype(jnp.bfloat16)
        first_pos = lax.axis_index("sq") * pos_local
        positions = first_pos + lax.broadcasted_iota(jnp.int32, (1, pos_local), 1)
        at_slot = (positions == cache_lens[:, None])[:, :, None]
        key_new = jnp.where(at_slot, key_val[:, None, :head_dim], k_cache)
        val_new = jnp.where(at_slot, key_val[:, None, head_dim:], v_cache)
        scores = jnp.einsum("bnd,btd->bnt", query, key_new, preferred_element_type=jnp.float32) * (head_dim ** -0.5)
        valid = (positions <= cache_lens[:, None])[:, None, :]
        scores = jnp.where(valid, scores, -1e30)
        local_max = jnp.max(scores, axis=-1, keepdims=True)
        global_max = lax.pmax(local_max, "sq")
        weights = jnp.where(valid, jnp.exp(scores - global_max), 0.0)
        denominator = lax.psum(jnp.sum(weights, axis=-1, keepdims=True), "sq")
        numerator = lax.psum(jnp.einsum("bnt,btd->bnd", weights.astype(jnp.bfloat16), val_new, preferred_element_type=jnp.float32), "sq")
        attended = (numerator / denominator).astype(jnp.bfloat16).reshape(batch, heads_local * head_dim)
        part_sum = jnp.dot(attended, w_out, preferred_element_type=jnp.float32)
        projected = lax.psum(part_sum, "tp")
        out_hidden = (hidden.astype(jnp.float32) + projected + b_out).astype(jnp.bfloat16)
        return out_hidden, key_new, val_new

    cache_spec = P("dp", "sq", None)
    row_spec = P("dp", None)
    in_specs = (row_spec, P("dp"), cache_spec, cache_spec, P(None), P(None), P(None, "tp"), P("tp"), P(None, None), P(None), P("tp", None), P(None))
    out_specs = (row_spec, cache_spec, cache_spec)
    return jax.shard_map(local_step, mesh=mesh, in_specs=in_specs, out_specs=out_specs, check_vma=False)
```

profile of v0, /device:TPU:97, one launch (start us, length us, event | category | flops | bytes accessed | tf_op | source)
XLA Modules:
  0.0 312.1 jit_solution(741860446331873235)
XLA Ops:
  7.2 0.0 copy-start
  7.2 0.0 copy-start.5
  7.2 0.0 copy-start.6
  7.2 0.0 copy-start.8
  7.2 0.1 all-reduce.3.cloned.1.call-start
  7.3 0.0 copy-start.2
  7.3 2.5 convert_reduce_fusion
  9.9 3.0 fusion.2
  12.9 0.0 copy-done
  12.9 0.0 copy-done.5
  12.9 0.0 copy-done.6
  12.9 0.0 copy-done.8
  12.9 0.0 copy-done.2
  12.9 0.0 copy-start.7
  13.0 1.3 fusion.19
  14.3 0.0 copy-done.7
  14.3 0.0 copy-start.4
  14.3 9.1 %fusion.11 = bf16[256,1536]{1,0:T(8,128)(2,1)S(1)} fusion(bf16[6144,1536]{1,0:T(8,128)(2,1)} %param.18, f32[1536]{0:T(1024)S(1)} %copy-done.7, bf16[256,6144]{1,0:T(8,128)(2,1)S(1)} %copy-done.2, f32[6144]{0:T(1024)S(1)} %copy-done.5, f32[6144]{0:T(1024)S(1)} %copy-done.6, f32[256]{0:T(256)S(1)} %add_rsqrt_fusion, f32[256]{0:T(256)S(1)} %broadcast_multiply_fusion), kind=kOutput, calls=%fused_computation.19 | convolution fusion | flops 4842061824 | bytes 22863872 | tf_op jit(solution)/shard_map/dot_general | solution.py:21
  23.5 0.3 copy.15
  23.8 1.0 copy.16
  24.8 0.0 copy-done.4
  24.8 0.1 broadcast_compare_fusion.1
  25.0 23.3 %broadcast_select_fusion.1 = (bf16[256,256,128]{2,1,0:T(8,128)(2,1)}, bf16[256,256,128]{2,1,0:T(8,128)(2,1)}) fusion(bf16[256,256,128]{2,1,0:T(8,128)(2,1)} %param.14, pred[256,256]{1,0:T(8,128)(4,1)S(1)} %get-tuple-element.8, bf16[256,128]{1,0:T(8,128)(2,1)S(1)} %get-tuple-element.3, bf16[256,256,128]{2,1,0:T(8,128)(2,1)} %param.15, ...), kind=kLoop, calls=%fused_computation.1 | loop fusion | flops 16777216 | bytes 67305472 | tf_op jit(solution)/shard_map/jit(_where)/select_n | solution.py:27
  48.3 12.2 %fusion.8 = (f32[256,12]{1,0:T(8,128)S(1)}, f32[256,12,256]{2,1,0:T(8,128)}) fusion(pred[256,256]{1,0:T(8,128)(4,1)S(1)} %get-tuple-element.7, bf16[256,12,128]{2,1,0:T(8,128)(2,1)S(1)} %copy.16, bf16[256,256,128]{2,1,0:T(8,128)(2,1)} %get-tuple-element.5), kind=kOutput, calls=%fused_computation.15 | convolution fusion | flops 203682816 | bytes 20787200 | tf_op jit(solution)/shard_map/bnd,btd->bnt/dot_general | solution.py:29
  60.4 25.4 %pmax.7 = f32[256,12]{1,0:T(8,128)S(1)} all-reduce(f32[256,12]{1,0:T(8,128)S(1)} %get-tuple-element.9), channel_id=1, replica_groups=mesh['dp'=1,'tp'=4,'sq'=8] {'sq'}, use_global_device_ids=true, to_apply=%region_3.4 | all-reduce | flops 3072 | bytes 24576 | tf_op jit(solution)/shard_map/pmax | solution.py:33
  85.9 11.2 %fusion.12 = f32[256,12,128]{2,1,0:T(8,128)} fusion(bf16[256,256,128]{2,1,0:T(8,128)(2,1)} %get-tuple-element.6, f32[256,12,256]{2,1,0:T(8,128)} %get-tuple-element.10, f32[256,12]{1,0:T(8,128)S(1)} %pmax.7, pred[256,256]{1,0:T(8,128)(4,1)S(1)} %get-tuple-element.7), kind=kOutput, calls=%fused_computation.20 | convolution fusion | flops 205258752 | bytes 21573632 | tf_op jit(solution)/shard_map/bnt,btd->bnd/dot_general | solution.py:36
  97.1 0.1 all-reduce.3.cloned.1.call-update
  97.1 0.1 all-reduce.5.cloned.1.call-start
  97.2 3.7 %fusion.9 = f32[256,12]{1,0:T(8,128)S(1)} fusion(f32[256,12,256]{2,1,0:T(8,128)} %get-tuple-element.10, f32[256,12]{1,0:T(8,128)S(1)} %pmax.7, pred[256,256]{1,0:T(8,128)(4,1)S(1)} %get-tuple-element.7), kind=kLoop, calls=%fused_computation.16 | loop fusion | flops 3929088 | bytes 3235840 | tf_op jit(solution)/shard_map/reduce_sum | solution.py:35
  100.9 25.8 %psum.22 = f32[256,12]{1,0:T(8,128)S(1)} all-reduce(f32[256,12]{1,0:T(8,128)S(1)} %fusion.9), channel_id=1, replica_groups=mesh['dp'=1,'tp'=4,'sq'=8] {'sq'}, use_global_device_ids=true, to_apply=%region_6.7 | all-reduce | flops 3072 | bytes 24576 | tf_op jit(solution)/shard_map/psum | solution.py:35
  126.7 32.8 %all-reduce.3.cloned.1.call-done = f32[256,12,128]{2,1,0:T(8,128)} async-done(((f32[256,12,128]{2,1,0:T(8,128)}), f32[256,12,128]{2,1,0:T(8,128)}) %all-reduce.3.cloned.1.call-update) | async-done | bytes 1572880 | tf_op jit(solution)/shard_map/psum | solution.py:36
  159.5 1.9 divide_convert_fusion
  161.5 0.9 copy.17
  162.4 13.5 %fusion.26 = f32[256,6144]{1,0:T(8,128)} fusion(bf16[256,1536]{0,1:T(8,128)(2,1)S(1)} %bitcast.9, bf16[1536,6144]{1,0:T(8,128)(2,1)} %param.22), kind=kOutput, calls=%fused_computation.38 | convolution fusion | flops 4831838208 | bytes 25952256 | tf_op jit(solution)/shard_map/dot_general | solution.py:38
  175.9 0.0 copy-start.3
  175.9 0.1 all-reduce.5.cloned.1.call-update
  175.9 0.0 copy-start.1
  175.9 123.0 %all-reduce.5.cloned.1.call-done = f32[256,6144]{1,0:T(8,128)} async-done(((f32[256,6144]{1,0:T(8,128)}), f32[256,6144]{1,0:T(8,128)}) %all-reduce.5.cloned.1.call-update) | async-done | bytes 6291472 | tf_op jit(solution)/shard_map/psum | solution.py:39
  298.9 0.0 copy-done.3
  298.9 6.3 %fusion.7 = bf16[256,6144]{1,0:T(8,128)(2,1)} fusion(f32[256,6144]{1,0:T(8,128)} %all-reduce.5.cloned.1.call-done, bf16[256,6144]{1,0:T(8,128)(2,1)} %param.12, f32[6144]{0:T(1024)S(1)} %copy-done.3), kind=kLoop, calls=%fused_computation.12 | loop fusion | flops 6291456 | bytes 12607488 | tf_op jit(solution)/shard_map/convert_element_type | solution.py:40
  305.2 0.0 copy-done.1
  (4 shorter events, 0.0 us)
Async XLA Ops:
  7.2 5.7 %copy-start = (bf16[6144,256]{1,0:T(8,128)(2,1)S(1)}, bf16[6144,256]{1,0:T(8,128)(2,1)}, u32[]{:S(2)}) copy-start(bf16[6144,256]{1,0:T(8,128)(2,1)} %param.20) | copy-start | bytes 9437188
  7.2 5.7 %copy-start.5 = (f32[6144]{0:T(1024)S(1)}, f32[6144]{0:T(1024)}, u32[]{:S(2)}) copy-start(f32[6144]{0:T(1024)} %param.17) | copy-start | bytes 73732
  7.2 5.7 %copy-start.6 = (f32[6144]{0:T(1024)S(1)}, f32[6144]{0:T(1024)}, u32[]{:S(2)}) copy-start(f32[6144]{0:T(1024)} %param.16) | copy-start | bytes 73732
  7.2 5.7 %copy-start.8 = (f32[256]{0:T(256)S(1)}, f32[256]{0:T(256)}, u32[]{:S(2)}) copy-start(f32[256]{0:T(256)} %param.21) | copy-start | bytes 3076
  7.2 152.3 %all-reduce.3.cloned.1.call-start = ((), (), s32[]{:S(2)}) async-start(), calls=%async_computation | async-start | bytes 4194304 | tf_op jit(solution)/shard_map/psum | solution.py:36
  7.3 5.6 %copy-start.2 = (bf16[256,6144]{1,0:T(8,128)(2,1)S(1)}, bf16[256,6144]{1,0:T(8,128)(2,1)}, u32[]{:S(2)}) copy-start(bf16[256,6144]{1,0:T(8,128)(2,1)} %param.12) | copy-start | bytes 9437188
  12.9 1.4 copy-start.7
  14.3 10.5 %copy-start.4 = (s32[256]{0:T(256)S(1)}, s32[256]{0:T(256)}, u32[]{:S(2)}) copy-start(s32[256]{0:T(256)} %param.13) | copy-start | bytes 3076
  97.1 201.8 %all-reduce.5.cloned.1.call-start = ((), (), s32[]{:S(2)}) async-start(), calls=%async_computation.1 | async-start | bytes 12582912 | tf_op jit(solution)/shard_map/psum | solution.py:39
  175.9 123.1 %copy-start.3 = (f32[6144]{0:T(1024)S(1)}, f32[6144]{0:T(1024)}, u32[]{:S(2)}) copy-start(f32[6144]{0:T(1024)} %param.23) | copy-start | bytes 73732
  175.9 129.3 %copy-start.1 = (bf16[6144,256]{1,0:T(8,128)(2,1)S(1)}, bf16[6144,256]{1,0:T(8,128)(2,1)}, u32[]{:S(2)}) copy-start(bf16[6144,256]{1,0:T(8,128)(2,1)} %param.20) | copy-start | bytes 9437188
Sparse Core Ops, SparseCore 0:
  97.2 62.2 all-reduce.2
  176.0 122.8 all-reduce.4
where the time goes:
time: 312 us
  waiting for transfers between devices  156 us (50%)
  blocking collectives  51.2 us (16%)
  matrix products  47.3 us (15%)
  other arithmetic  41 us (13%)
  between operations  14.3 us (5%)
    psum x1, waiting for transfers between devices, local_step(): projected = lax.psum(part_sum, 'tp')  123 us
    psum x1, waiting for transfers between devices, local_step(): lax.psum(jnp.einsum('bnt,btd->bnd', weights.astype(jnp.bfloat16), val_new...  32.8 us
    psum x1, blocking collectives, local_step(): denominator = lax.psum(jnp.sum(weights, axis=-1, keepdims=True), 'sq')  25.8 us
    pmax x1, blocking collectives, local_step(): global_max = lax.pmax(local_max, 'sq')  25.4 us
    select_n x1, other arithmetic, local_step(): key_new = jnp.where(at_slot, key_val[:, None, :head_dim], k_cache)  23.3 us
    dot_general x1, matrix products, local_step(): part_sum = jnp.dot(attended, w_out, preferred_element_type=jnp.float32)  13.5 us
    dot_general x1, matrix products, local_step(): jnp.einsum('bnd,btd->bnt', query, key_new, preferred_element_type=jnp.flo...  12.2 us
    dot_general x1, matrix products, local_step(): jnp.einsum('bnt,btd->bnd', weights.astype(jnp.bfloat16), val_new, preferr...  11.2 us
  transfers between devices with their start and end apart: 2, of which 2 were waited for; matrix products, arithmetic and copies ran while one was open for 1% of the time, Pallas kernels for 0%

commit v1 on v0

--- a/solution.py
+++ b/solution.py
@@ -1,7 +1,15 @@
+import functools
+
 import jax
 import jax.numpy as jnp
 from jax import lax
+from jax.experimental import pallas as pl
+from jax.experimental.pallas import tpu as pltpu
 from jax.sharding import PartitionSpec as P
+
+MESH = pl.DeviceIdType.MESH
+LANES = 128
+NEG = -1e30
 
 
 def layer_norm(x_rows, ln_gain, ln_bias):
@@ -13,7 +21,281 @@
     return (normed * ln_gain + ln_bias).astype(jnp.bfloat16)
 
 
+def merge_into(dst, part_a, part_b, heads):
+    width = heads * LANES
+    stat_a, stat_b = part_a[:, width:], part_b[:, width:]
+    top = jnp.maximum(stat_a, stat_b)
+    exp_a, exp_b = jnp.exp(stat_a - top), jnp.exp(stat_b - top)
+    sums = stat_a * pltpu.roll(exp_a, 64, 1) + stat_b * pltpu.roll(exp_b, 64, 1)
+    lane = lax.broadcasted_iota(jnp.int32, top.shape, 1)
+    dst[:, width:] = jnp.where(lane < 64, top, sums)
+    for n in range(heads):
+        cols = slice(n * LANES, (n + 1) * LANES)
+        dst[:, cols] = part_a[:, cols] * exp_a[:, n : n + 1] + part_b[:, cols] * exp_b[:, n : n + 1]
+
+
+def finish_kernel(
+    dims,
+    part_ref,
+    b_out_ref,
+    hidden_ref,
+    w_out_ref,
+    out_ref,
+    w_buf,
+    pair_buf,
+    merge_buf,
+    x_buf,
+    att_buf,
+    proj_buf,
+    y_buf,
+    hid_buf,
+    gather_buf,
+    w_sem,
+    hid_sem,
+    pair_send,
+    pair_recv,
+    x_send,
+    x_recv,
+    y_send,
+    y_recv,
+    g_send,
+    g_recv,
+    d_send,
+    d_recv,
+):
+    nx, ny, heads, rows, cols = dims
+    half = cols // 2
+    width = heads * LANES
+    sq = lax.axis_index("sq")
+    y = lax.axis_index("tp")
+    x = sq // 2
+    core = sq % 2
+    step = 1 - 2 * core
+
+    def wrap(value, size):
+        return lax.rem(value + 2 * size, size)
+
+    x_fwd, x_bwd, x_opp = wrap(x + step, nx), wrap(x - step, nx), wrap(x + 2, nx)
+    y_fwd, y_bwd, y_opp = wrap(y + step, ny), wrap(y - step, ny), wrap(y + 2, ny)
+    to_pair = {"sq": x * 2 + 1 - core}
+    to_x_fwd, to_x_bwd = {"sq": x_fwd * 2 + core}, {"sq": x_bwd * 2 + core}
+    to_y_fwd, to_y_bwd = {"tp": y_fwd}, {"tp": y_bwd}
+
+    barrier = pltpu.get_barrier_semaphore()
+    for peer in (to_pair, to_x_fwd, to_x_bwd, to_y_fwd, to_y_bwd):
+        pl.semaphore_signal(barrier, inc=1, device_id=peer, device_id_type=MESH)
+
+    y_order = (y_opp, y_bwd, y_fwd, y)
+    w_copies = []
+    for k, target in enumerate(y_order):
+        src = w_out_ref.at[:, pl.ds(pl.multiple_of(target * cols, cols), cols)]
+        w_copies.append(pltpu.make_async_copy(src, w_buf.at[k], w_sem.at[k]))
+    my_row = pl.multiple_of(sq * rows, rows)
+    my_col = pl.multiple_of(y * cols, cols)
+    hid_copy = pltpu.make_async_copy(hidden_ref.at[pl.ds(my_row, rows), pl.ds(my_col, cols)], hid_buf, hid_sem)
+    pl.semaphore_wait(barrier, 5)
+
+    sends = []
+
+    def send(src, dst, ssem, rsem, peer):
+        copy = pltpu.make_async_remote_copy(
+            src_ref=src, dst_ref=dst, send_sem=ssem, recv_sem=rsem, device_id=peer, device_id_type=MESH
+        )
+        copy.start()
+        sends.append(copy)
+        return copy
+
+    def part_rows(xt, ct):
+        return pl.ds(pl.multiple_of((xt * 2 + ct) * rows, rows), rows)
+
+    pair = []
+    for k, xt in enumerate((x_opp, x_fwd, x_bwd, x)):
+        pair.append(send(part_ref.at[part_rows(xt, 1 - core), :], pair_buf.at[k], pair_send.at[k], pair_recv.at[k], to_pair))
+    for copy in w_copies:
+        copy.start()
+    hid_copy.start()
+
+    pair[0].wait_recv()
+    merge_into(merge_buf.at[0], part_ref[part_rows(x_opp, core), :], pair_buf[0], heads)
+    x_o = send(merge_buf.at[0], x_buf.at[0], x_send.at[0], x_recv.at[0], to_x_fwd)
+    pair[1].wait_recv()
+    merge_into(merge_buf.at[1], part_ref[part_rows(x_bwd, core), :], pair_buf[1], heads)
+    x_b = send(merge_buf.at[1], x_buf.at[1], x_send.at[1], x_recv.at[1], to_x_bwd)
+    pair[2].wait_recv()
+    merge_into(merge_buf.at[2], part_ref[part_rows(x_fwd, core), :], pair_buf[2], heads)
+    x_o.wait_recv()
+    merge_into(merge_buf.at[3], merge_buf[2], x_buf[0], heads)
+    x_a = send(merge_buf.at[3], x_buf.at[2], x_send.at[2], x_recv.at[2], to_x_fwd)
+    pair[3].wait_recv()
+    merge_into(merge_buf.at[4], part_ref[part_rows(x, core), :], pair_buf[3], heads)
+    x_b.wait_recv()
+    merge_into(merge_buf.at[5], merge_buf[4], x_buf[1], heads)
+    x_a.wait_recv()
+    merge_into(merge_buf.at[6], merge_buf[5], x_buf[2], heads)
+    stat = merge_buf[6, :, width:]
+    for n in range(heads):
+        block = slice(n * LANES, (n + 1) * LANES)
+        att_buf[:, block] = (merge_buf[6, :, block] / stat[:, 64 + n : 65 + n]).astype(jnp.bfloat16)
+
+    for copy in w_copies:
+        copy.wait()
+    hid_copy.wait()
+
+    def project(k, h):
+        return jnp.dot(att_buf[...], w_buf[k, :, h * half : (h + 1) * half], preferred_element_type=jnp.float32)
+
+    y_o, y_b, y_a = [None, None], [None, None], [None, None]
+    for h in range(2):
+        proj_buf[0, h] = project(0, h)
+        y_o[h] = send(proj_buf.at[0, h], y_buf.at[0, h], y_send.at[0, h], y_recv.at[0, h], to_y_fwd)
+    for h in range(2):
+        proj_buf[1, h] = project(1, h)
+        y_b[h] = send(proj_buf.at[1, h], y_buf.at[1, h], y_send.at[1, h], y_recv.at[1, h], to_y_bwd)
+        fwd_part = project(2, h)
+        y_o[h].wait_recv()
+        proj_buf[2, h] = fwd_part + y_buf[0, h]
+        y_a[h] = send(proj_buf.at[2, h], y_buf.at[2, h], y_send.at[2, h], y_recv.at[2, h], to_y_fwd)
+        own_cols = pl.ds(pl.multiple_of(y * cols + h * half, half), half)
+        own = project(3, h) + hid_buf[:, h * half : (h + 1) * half].astype(jnp.float32) + b_out_ref[:, own_cols]
+        proj_buf[3, h] = own
+
+    def place(xt, yt, ct, h):
+        row = pl.multiple_of((xt * 2 + ct) * rows, rows)
+        col = pl.multiple_of(yt * cols + h * half, half)
+        return pl.ds(row, rows), pl.ds(col, half)
+
+    xs = (x, x_bwd, x_fwd, x_opp)
+    ys = (y, y_bwd, y_fwd, y_opp)
+    x_peers, y_peers = (to_x_fwd, to_x_bwd), (to_y_fwd, to_y_bwd)
+    gathers = {}
+    pairs = {}
+
+    def spot(h, first, second, ct=None):
+        ct = core if ct is None else ct
+        if h == 0:
+            return place(xs[first], ys[second], ct, h)
+        return place(xs[second], ys[first], ct, h)
+
+    def piece(h, first, second):
+        return gather_buf.at[spot(h, first, second)]
+
+    def ring_send(h, first, second, slot, phase):
+        peers = (x_peers, y_peers) if h == 0 else (y_peers, x_peers)
+        peer = peers[phase][1 if slot == 2 else 0]
+        index = slot - 1 if phase == 0 else 3 + first * 3 + slot - 1
+        key = (h, phase, first if phase else 0, slot)
+        ref = piece(h, first, second)
+        gathers[key] = send(ref, ref, g_send.at[h, index], g_recv.at[h, index], peer)
+
+    def pair_forward(h, first, second):
+        ref = piece(h, first, second)
+        index = first * 4 + second
+        pairs[(h, first, second)] = send(ref, ref, d_send.at[h, index], d_recv.at[h, index], to_pair)
+
+    def convert(where):
+        out_ref[where] = gather_buf[where].astype(jnp.bfloat16)
+
+    def mirrored(slot):
+        return (0, 2, 1, 3)[slot]
+
+    todo = []
+
+    def drain(limit):
+        while len(todo) > limit:
+            h, first, second = todo.pop(0)
+            pairs[(h, first, second)].wait_recv()
+            convert(spot(h, mirrored(first), mirrored(second), 1 - core))
+
+    def have(h, first, second):
+        pair_forward(h, first, second)
+        convert(spot(h, first, second))
+        todo.append((h, first, second))
+        drain(2)
+
+    for h in range(2):
+        y_b[h].wait_recv()
+        part = proj_buf[3, h] + y_buf[1, h]
+        y_a[h].wait_recv()
+        gather_buf[spot(h, 0, 0)] = part + y_buf[2, h]
+        ring_send(h, 0, 0, 1, 0)
+        ring_send(h, 0, 0, 2, 0)
+        pair_forward(h, 0, 0)
+    for h in range(2):
+        ring_send(h, 0, 0, 1, 1)
+        ring_send(h, 0, 0, 2, 1)
+        convert(spot(h, 0, 0))
+        todo.append((h, 0, 0))
+
+    def arrived(h, first, second):
+        if second == 0:
+            gathers[(h, 0, 0, first)].wait_recv()
+            if first == 1:
+                ring_send(h, 1, 0, 3, 0)
+            ring_send(h, first, 0, 1, 1)
+            ring_send(h, first, 0, 2, 1)
+        else:
+            gathers[(h, 1, first, second)].wait_recv()
+            if second == 1:
+                ring_send(h, first, 1, 3, 1)
+        have(h, first, second)
+
+    order = [(1, 0), (2, 0), (0, 1), (0, 2), (3, 0), (1, 1), (0, 3), (2, 1), (1, 2), (1, 3), (2, 2), (3, 1), (2, 3), (3, 2), (3, 3)]
+    for first, second in order:
+        for h in range(2):
+            arrived(h, first, second)
+    drain(0)
+    for copy in sends:
+        copy.wait_send()
+
+
+def finish(parts, hidden, w_out, b_out, nx, ny):
+    batch, width = parts.shape
+    heads = width // LANES - 1
+    depth, d_model = w_out.shape
+    rows, cols = batch // (2 * nx), d_model // ny
+    half = cols // 2
+    f32, dma = jnp.float32, pltpu.SemaphoreType.DMA
+    return pl.pallas_call(
+        functools.partial(finish_kernel, (nx, ny, heads, rows, cols)),
+        out_shape=jax.ShapeDtypeStruct((batch, d_model), jnp.bfloat16),
+        in_specs=[
+            pl.BlockSpec(memory_space=pltpu.VMEM),
+            pl.BlockSpec(memory_space=pltpu.VMEM),
+            pl.BlockSpec(memory_space=pl.ANY),
+            pl.BlockSpec(memory_space=pl.ANY),
+        ],
+        out_specs=pl.BlockSpec(memory_space=pltpu.VMEM),
+        scratch_shapes=[
+            pltpu.VMEM((4, depth, cols), jnp.bfloat16),
+            pltpu.VMEM((4, rows, width), f32),
+            pltpu.VMEM((7, rows, width), f32),
+            pltpu.VMEM((3, rows, width), f32),
+            pltpu.VMEM((rows, heads * LANES), jnp.bfloat16),
+            pltpu.VMEM((4, 2, rows, half), f32),
+            pltpu.VMEM((3, 2, rows, half), f32),
+            pltpu.VMEM((rows, cols), jnp.bfloat16),
+            pltpu.VMEM((batch, d_model), f32),
+            dma((4,)),
+            dma,
+            dma((4,)),
+            dma((4,)),
+            dma((3,)),
+            dma((3,)),
+            dma((3, 2)),
+            dma((3, 2)),
+            dma((2, 15)),
+            dma((2, 15)),
+            dma((2, 16)),
+            dma((2, 16)),
+        ],
+        compiler_params=pltpu.CompilerParams(collective_id=0, has_side_effects=True, vmem_limit_bytes=48 * 1024 * 1024),
+        name="finish",
+    )(parts, b_out.reshape(1, d_model), hidden, w_out)
+
+
 def solution(mesh):
+    nx, ny = mesh.shape["sq"] // 2, mesh.shape["tp"]
+
     def local_step(hidden, cache_lens, k_cache, v_cache, ln_gain, ln_bias, w_query, b_query, w_kv, b_kv, w_out, b_out):
         batch, pos_local, head_dim = k_cache.shape
         heads_local = w_query.shape[1] // head_dim
@@ -28,16 +310,16 @@
         val_new = jnp.where(at_slot, key_val[:, None, head_dim:], v_cache)
         scores = jnp.einsum("bnd,btd->bnt", query, key_new, preferred_element_type=jnp.float32) * (head_dim ** -0.5)
         valid = (positions <= cache_lens[:, None])[:, None, :]
-        scores = jnp.where(valid, scores, -1e30)
+        scores = jnp.where(valid, scores, NEG)
         local_max = jnp.max(scores, axis=-1, keepdims=True)
-        global_max = lax.pmax(local_max, "sq")
-        weights = jnp.where(valid, jnp.exp(scores - global_max), 0.0)
-        denominator = lax.psum(jnp.sum(weights, axis=-1, keepdims=True), "sq")
-        numerator = lax.psum(jnp.einsum("bnt,btd->bnd", weights.astype(jnp.bfloat16), val_new, preferred_element_type=jnp.float32), "sq")
-        attended = (numerator / denominator).astype(jnp.bfloat16).reshape(batch, heads_local * head_dim)
-        part_sum = jnp.dot(attended, w_out, preferred_element_type=jnp.float32)
-        projected = lax.psum(part_sum, "tp")
-        out_hidden = (hidden.astype(jnp.float32) + projected + b_out).astype(jnp.bfloat16)
+        weights = jnp.where(valid, jnp.exp(scores - local_max), 0.0)
+        local_sum = jnp.sum(weights, axis=-1)
+        numerator = jnp.einsum("bnt,btd->bnd", weights.astype(jnp.bfloat16), val_new, preferred_element_type=jnp.float32)
+        pad = ((0, 0), (0, 64 - heads_local))
+        parts = jnp.concatenate(
+            [numerator.reshape(batch, heads_local * head_dim), jnp.pad(local_max[..., 0], pad), jnp.pad(local_sum, pad)], axis=1
+        )
+        out_hidden = finish(parts, hidden, w_out, b_out, nx, ny)
         return out_hidden, key_new, val_new
 
     cache_spec = P("dp", "sq", None)

time: 312 us -> 126 us (0.40)
  waiting for transfers between devices: 156 us -> 0 us
  Pallas kernels: 0 us -> 54 us
  blocking collectives: 51.2 us -> 0 us
  matrix products: 47.3 us -> 30.1 us
  between operations: 14.3 us -> 0.86 us
  other arithmetic: 41 us -> 30.9 us
  local copies, waits for them, and re-layouts: 2.23 us -> 9.79 us
    psum x2 -> x0, waiting for transfers between devices: 156 us -> none  [the longest x1 123 us: local_step(): projected = lax.psum(part_sum, 'tp')]
    pallas_call x0 -> x1, Pallas kernels: none -> 54 us  [finish(): pl.pallas_call(functools.partial(finish_kernel, (nx, ny, heads, rows, col...]
    psum x1 -> x0, blocking collectives: 25.8 us -> none  [local_step(): denominator = lax.psum(jnp.sum(weights, axis=-1, keepdims=True), 'sq')]
    pmax x1 -> x0, blocking collectives: 25.4 us -> none  [local_step(): global_max = lax.pmax(local_max, 'sq')]
    dot_general x1 -> x0, matrix products: 13.5 us -> none  [local_step(): part_sum = jnp.dot(attended, w_out, preferred_element_type=jnp.float32)]
    convert_element_type x2 -> x0, other arithmetic: 8.22 us -> none  [the longest x1 6.28 us: local_step(): (hidden.astype(jnp.float32) + projected + b_out).astype(jnp.bfloat16)]
    dot_general x1, matrix products: 11.2 us -> 7.29 us  [local_step(): jnp.einsum('bnt,btd->bnd', weights.astype(jnp.bfloat16), val_new, preferr...]
    unnamed x18 -> x23, local copies, waits for them, and re-layouts: 0.05 us -> 3.54 us
  transfers between devices with their start and end apart: 2 -> 0, of which waited for: 2 -> 0; matrix products, arithmetic and copies ran while one was open for 1% -> 0% of each run, Pallas kernels for 0% -> 0%
where the time goes in v1:
time: 126 us
  Pallas kernels  54 us (43%)
  other arithmetic  30.9 us (25%)
  matrix products  30.1 us (24%)
  local copies, waits for them, and re-layouts  9.79 us (8%)
    pallas_call x1, Pallas kernels, finish(): pl.pallas_call(functools.partial(finish_kernel, (nx, ny, heads, rows, col...  54 us
    select_n x1, other arithmetic, local_step(): key_new = jnp.where(at_slot, key_val[:, None, :head_dim], k_cache)  23.3 us
    dot_general x1, matrix products, local_step(): jnp.einsum('bnd,btd->bnt', query, key_new, preferred_element_type=jnp.flo...  12.2 us
    dot_general x1, matrix products, local_step(): jnp.dot(normed, w_query, preferred_element_type=jnp.float32) + b_query  9.33 us
    dot_general x1, matrix products, local_step(): jnp.einsum('bnt,btd->bnd', weights.astype(jnp.bfloat16), val_new, preferr...  7.29 us
    reduce_sum x1, other arithmetic, local_step(): local_sum = jnp.sum(weights, axis=-1)  3.9 us
    unnamed x23, local copies, waits for them, and re-layouts  3.54 us
    reduce_sum x1, other arithmetic, layer_norm(): mean_val = jnp.mean(x_wide, axis=-1, keepdims=True)  2.57 us

profile of v1, /device:TPU:97, one launch (start us, length us, event | category | flops | bytes accessed | tf_op | source)
XLA Modules:
  0.0 125.7 jit_solution(12473251165213232742)
XLA Ops:
  0.6 0.0 copy-start
  0.6 0.0 copy-start.10
  0.7 0.0 copy-start.6
  0.7 0.0 copy-start.5
  0.7 0.0 copy-start.7
  0.7 0.0 copy-start.8
  0.7 2.6 %convert_reduce_fusion = f32[256]{0:T(256)S(1)} fusion(bf16[256,6144]{1,0:T(8,128)(2,1)} %hidden_ref.1), kind=kLoop, calls=%fused_computation.3 | loop fusion | flops 3145472 | bytes 3146752 | tf_op jit(solution)/shard_map/reduce_sum | solution.py:17
  3.3 0.4 copy-done.5
  3.7 1.0 fusion.2
  4.6 0.0 copy-done.6
  4.6 0.1 broadcast_compare_fusion.1
  4.8 0.0 copy-done
  4.8 0.0 copy-done.10
  4.8 0.0 copy-done.7
  4.8 0.0 copy-done.8
  4.8 0.0 copy-start.9
  4.8 1.3 %fusion.17 = bf16[256,256]{1,0:T(8,128)(2,1)S(1)} fusion(bf16[6144,256]{1,0:T(8,128)(2,1)S(1)} %copy-done, f32[256]{0:T(256)S(1)} %copy-done.10, bf16[256,6144]{1,0:T(8,128)(2,1)S(1)} %copy-done.5, f32[6144]{0:T(1024)S(1)} %copy-done.7, f32[6144]{0:T(1024)S(1)} %copy-done.8, f32[256]{0:T(256)S(1)} %add_rsqrt_fusion, f32[256]{0:T(256)S(1)} %broadcast_multiply_fusion), kind=kOutput, calls=%fused_computation.24 | convolution fusion | flops 814874624 | bytes 6474752 | tf_op jit(solution)/shard_map/dot_general | solution.py:305
  6.2 0.0 copy-done.9
  6.2 9.3 %fusion.9 = bf16[256,1536]{1,0:T(8,128)(2,1)S(1)} fusion(bf16[6144,1536]{1,0:T(8,128)(2,1)} %param.18, f32[1536]{0:T(1024)S(1)} %copy-done.9, bf16[256,6144]{1,0:T(8,128)(2,1)S(1)} %copy-done.5, f32[6144]{0:T(1024)S(1)} %copy-done.7, f32[6144]{0:T(1024)S(1)} %copy-done.8, f32[256]{0:T(256)S(1)} %add_rsqrt_fusion, f32[256]{0:T(256)S(1)} %broadcast_multiply_fusion), kind=kOutput, calls=%fused_computation.16 | convolution fusion | flops 4842061824 | bytes 22863872 | tf_op jit(solution)/shard_map/dot_general | solution.py:303
  15.6 0.3 copy.15
  15.8 1.0 copy.16
  16.9 23.3 %broadcast_select_fusion.1 = (bf16[256,256,128]{2,1,0:T(8,128)(2,1)}, bf16[256,256,128]{2,1,0:T(8,128)(2,1)}) fusion(bf16[256,256,128]{2,1,0:T(8,128)(2,1)} %param.14, pred[256,256]{1,0:T(8,128)(4,1)S(1)} %get-tuple-element.8, bf16[256,128]{1,0:T(8,128)(2,1)S(1)} %get-tuple-element.3, bf16[256,256,128]{2,1,0:T(8,128)(2,1)} %param.15, ...), kind=kLoop, calls=%fused_computation.1 | loop fusion | flops 16777216 | bytes 67305472 | tf_op jit(solution)/shard_map/jit(_where)/select_n | solution.py:309
  40.2 12.2 %fusion.6 = (f32[256,12]{1,0:T(8,128)S(1)}, f32[256,12,256]{2,1,0:T(8,128)}) fusion(pred[256,256]{1,0:T(8,128)(4,1)S(1)} %get-tuple-element.7, bf16[256,12,128]{2,1,0:T(8,128)(2,1)S(1)} %copy.16, bf16[256,256,128]{2,1,0:T(8,128)(2,1)} %get-tuple-element.15), kind=kOutput, calls=%fused_computation.12 | convolution fusion | flops 203682816 | bytes 20787200 | tf_op jit(solution)/shard_map/bnd,btd->bnt/dot_general | solution.py:311
  52.4 0.0 copy-start.4
  52.4 3.9 %fusion.7 = f32[256,12]{1,0:T(8,128)S(1)} fusion(f32[256,12,256]{2,1,0:T(8,128)} %get-tuple-element.10, f32[256,12]{1,0:T(8,128)S(1)} %get-tuple-element.9, pred[256,256]{1,0:T(8,128)(4,1)S(1)} %get-tuple-element.7), kind=kLoop, calls=%fused_computation.13 | loop fusion | flops 3929088 | bytes 3235840 | tf_op jit(solution)/shard_map/reduce_sum | solution.py:316
  56.3 0.0 copy-done.4
  56.3 7.3 %fusion.10 = f32[256,12,128]{2,1,0:T(8,128)S(1)} fusion(bf16[256,256,128]{2,1,0:T(8,128)(2,1)} %get-tuple-element.16, f32[256,12,256]{2,1,0:T(8,128)S(1)} %copy-done.4, f32[256,12]{1,0:T(8,128)S(1)} %get-tuple-element.9, pred[256,256]{1,0:T(8,128)(4,1)S(1)} %get-tuple-element.7), kind=kOutput, calls=%fused_computation.17 | convolution fusion | flops 205258752 | bytes 21573632 | tf_op jit(solution)/shard_map/bnt,btd->bnd/dot_general | solution.py:317
  63.6 1.6 %copy.17 = f32[256,12,128]{0,2,1:T(8,128)} copy(f32[256,12,128]{2,1,0:T(8,128)S(1)} %fusion.10) | data formatting | bytes 3145728 | tf_op jit(solution)/shard_map/bnt,btd->bnd/dot_general | solution.py:317
  65.2 0.0 copy-start.3
  65.2 1.9 %copy.18 = f32[256,1536]{1,0:T(8,128)S(1)} copy(f32[256,1536]{0,1:T(8,128)} %bitcast.9) | data formatting | bytes 3145728 | tf_op jit(solution)/shard_map/reshape | solution.py:320
  67.1 1.4 %concatenate.3.part_ref = f32[256,1664]{1,0:T(8,128)} concatenate(f32[256,1536]{1,0:T(8,128)S(1)} %copy.18, f32[256,64]{1,0:T(8,128)S(1)} %pad.7, f32[256,64]{1,0:T(8,128)S(1)} %pad.8), dimensions={1} | concatenate | bytes 3407872 | tf_op jit(solution)/shard_map/concatenate | solution.py:319
  68.5 0.0 copy-done.3
  68.5 0.0 copy-start.2
  68.5 1.5 %copy-done.2 = f32[256,1664]{1,0:T(8,128)S(1)} copy-done((f32[256,1664]{1,0:T(8,128)S(1)}, f32[256,1664]{1,0:T(8,128)}, u32[]{:S(2)}) %copy-start.2) | copy-done | bytes 1703960
  70.0 0.0 copy-start.1
  70.0 54.0 %finish.1 = bf16[256,6144]{1,0:T(8,128)(2,1)S(1)} custom-call(f32[256,1664]{1,0:T(8,128)S(1)} %copy-done.2, f32[1,6144]{1,0:T(1,128)S(1)} %bitcast.8, bf16[256,6144]{1,0:T(8,128)(2,1)} %hidden_ref.1, bf16[1536,6144]{1,0:T(8,128)(2,1)} %w_out_ref.1), custom_call_target="tpu_custom_call" | custom-call | tf_op jit(solution)/shard_map/finish/pallas_call | solution.py:258
  124.0 1.7 %copy.20 = bf16[256,6144]{1,0:T(8,128)(2,1)} copy(bf16[256,6144]{1,0:T(8,128)(2,1)S(1)} %finish.1) | data formatting | bytes 6291456
  125.7 0.0 copy-done.1
  (6 shorter events, 0.1 us)
Async XLA Ops:
  0.6 4.2 %copy-start = (bf16[6144,256]{1,0:T(8,128)(2,1)S(1)}, bf16[6144,256]{1,0:T(8,128)(2,1)}, u32[]{:S(2)}) copy-start(bf16[6144,256]{1,0:T(8,128)(2,1)} %param.20) | copy-start | bytes 9437188
  0.6 4.2 %copy-start.10 = (f32[256]{0:T(256)S(1)}, f32[256]{0:T(256)}, u32[]{:S(2)}) copy-start(f32[256]{0:T(256)} %param.21) | copy-start | bytes 3076
  0.7 4.0 %copy-start.6 = (s32[256]{0:T(256)S(1)}, s32[256]{0:T(256)}, u32[]{:S(2)}) copy-start(s32[256]{0:T(256)} %param.13) | copy-start | bytes 3076
  0.7 3.0 %copy-start.5 = (bf16[256,6144]{1,0:T(8,128)(2,1)S(1)}, bf16[256,6144]{1,0:T(8,128)(2,1)}, u32[]{:S(2)}) copy-start(bf16[256,6144]{1,0:T(8,128)(2,1)} %hidden_ref.1) | copy-start | bytes 9437188
  0.7 4.1 %copy-start.7 = (f32[6144]{0:T(1024)S(1)}, f32[6144]{0:T(1024)}, u32[]{:S(2)}) copy-start(f32[6144]{0:T(1024)} %param.17) | copy-start | bytes 73732
  0.7 4.1 %copy-start.8 = (f32[6144]{0:T(1024)S(1)}, f32[6144]{0:T(1024)}, u32[]{:S(2)}) copy-start(f32[6144]{0:T(1024)} %param.16) | copy-start | bytes 73732
  4.8 1.4 %copy-start.9 = (f32[1536]{0:T(1024)S(1)}, f32[1536]{0:T(1024)}, u32[]{:S(2)}) copy-start(f32[1536]{0:T(1024)} %param.19) | copy-start | bytes 18436
  52.4 3.9 %copy-start.4 = (f32[256,12,256]{2,1,0:T(8,128)S(1)}, f32[256,12,256]{2,1,0:T(8,128)}, u32[]{:S(2)}) copy-start(f32[256,12,256]{2,1,0:T(8,128)} %get-tuple-element.10) | copy-start | bytes 9437188
  65.2 3.3 %copy-start.3 = (f32[6144]{0:T(1024)S(1)}, f32[6144]{0:T(1024)}, u32[]{:S(2)}) copy-start(f32[6144]{0:T(1024)} %param.23) | copy-start | bytes 73732
  68.5 1.5 %copy-start.2 = (f32[256,1664]{1,0:T(8,128)S(1)}, f32[256,1664]{1,0:T(8,128)}, u32[]{:S(2)}) copy-start(f32[256,1664]{1,0:T(8,128)} %concatenate.3.part_ref) | copy-start | bytes 5111812
  70.0 55.7 %copy-start.1 = (bf16[6144,256]{1,0:T(8,128)(2,1)S(1)}, bf16[6144,256]{1,0:T(8,128)(2,1)}, u32[]{:S(2)}) copy-start(bf16[6144,256]{1,0:T(8,128)(2,1)} %param.20) | copy-start | bytes 9437188

commit v2 on v1

--- a/solution.py
+++ b/solution.py
@@ -9,16 +9,6 @@
 
 MESH = pl.DeviceIdType.MESH
 LANES = 128
-NEG = -1e30
-
-
-def layer_norm(x_rows, ln_gain, ln_bias):
-    x_wide = x_rows.astype(jnp.float32)
-    mean_val = jnp.mean(x_wide, axis=-1, keepdims=True)
-    centered = x_wide - mean_val
-    variance = jnp.mean(centered * centered, axis=-1, keepdims=True)
-    normed = centered * lax.rsqrt(variance + 1e-5)
-    return (normed * ln_gain + ln_bias).astype(jnp.bfloat16)
 
 
 def merge_into(dst, part_a, part_b, heads):
@@ -293,32 +283,207 @@
     )(parts, b_out.reshape(1, d_model), hidden, w_out)
 
 
+ATTEND_SEQS = 16
+WIDE = 256
+W_SLOTS = 5
+
+
+def attend_kernel(
+    dims,
+    lens_ref,
+    hidden_ref,
+    gain_ref,
+    bias_ref,
+    b_query_ref,
+    b_kv_ref,
+    w_query_ref,
+    w_kv_ref,
+    k_ref,
+    v_ref,
+    part_ref,
+    k_out_ref,
+    v_out_ref,
+    h_buf,
+    w_buf,
+    q_buf,
+    kv_buf,
+    k_buf,
+    v_buf,
+    o_buf,
+    h_sem,
+    w_sem,
+    in_sem,
+    out_sem,
+):
+    batch, d_model, heads, pos_local = dims
+    hd, seqs = LANES, ATTEND_SEQS
+    steps = batch // seqs
+    blocks = heads * hd // WIDE
+    first_pos = lax.axis_index("sq") * pos_local
+    scale = hd ** -0.5
+    lowest = float(jnp.finfo(jnp.float32).min)
+
+    def w_copy(k):
+        src = w_kv_ref if k == 0 else w_query_ref.at[:, (k - 1) * WIDE : k * WIDE]
+        return pltpu.make_async_copy(src, w_buf.at[k % W_SLOTS], w_sem.at[k])
+
+    def rows_of(c):
+        return pl.ds(pl.multiple_of(c * seqs, seqs), seqs)
+
+    def read(c):
+        return (
+            pltpu.make_async_copy(k_ref.at[rows_of(c)], k_buf.at[rows_of(c)], in_sem.at[0, c]),
+            pltpu.make_async_copy(v_ref.at[rows_of(c)], v_buf.at[rows_of(c)], in_sem.at[1, c]),
+        )
+
+    def write(c):
+        return (
+            pltpu.make_async_copy(k_buf.at[rows_of(c)], k_out_ref.at[rows_of(c)], out_sem.at[0, c]),
+            pltpu.make_async_copy(v_buf.at[rows_of(c)], v_out_ref.at[rows_of(c)], out_sem.at[1, c]),
+        )
+
+    h_copy = pltpu.make_async_copy(hidden_ref, h_buf, h_sem)
+    h_copy.start()
+    for k in range(W_SLOTS):
+        w_copy(k).start()
+    q_buf[...] = jnp.zeros_like(q_buf)
+    h_copy.wait()
+
+    def norm_rows(r, _):
+        at = pl.ds(pl.multiple_of(r * 16, 16), 16)
+        x_wide = h_buf[at, :].astype(jnp.float32)
+        mean_val = jnp.sum(x_wide, axis=-1, keepdims=True) * (1.0 / d_model)
+        centered = x_wide - mean_val
+        variance = jnp.sum(centered * centered, axis=-1, keepdims=True) * (1.0 / d_model)
+        normed = centered * lax.rsqrt(variance + 1e-5)
+        h_buf[at, :] = (normed * gain_ref[...] + bias_ref[...]).astype(jnp.bfloat16)
+        return 0
+
+    lax.fori_loop(0, batch // 16, norm_rows, 0)
+
+    for k in range(blocks + 1):
+        w_copy(k).wait()
+        acc = jnp.dot(h_buf[...], w_buf[k % W_SLOTS], preferred_element_type=jnp.float32)
+        if k == 0:
+            acc = (acc + b_kv_ref[...]).astype(jnp.bfloat16).astype(jnp.float32)
+            kv_buf[0] = acc[:, :hd]
+            kv_buf[1] = acc[:, hd:]
+        else:
+            acc = (acc + b_query_ref[:, (k - 1) * WIDE : k * WIDE]).astype(jnp.bfloat16).astype(jnp.float32)
+            for e in range(WIDE // hd):
+                n = (k - 1) * (WIDE // hd) + e
+                q_buf[pl.ds(n, batch, stride=16), :] = acc[:, e * hd : (e + 1) * hd]
+        if k + W_SLOTS <= blocks:
+            w_copy(k + W_SLOTS).start()
+        if k + W_SLOTS == blocks:
+            for c in range(steps):
+                for copy in read(c):
+                    copy.start()
+
+    def attend(c, _):
+        for copy in read(c):
+            copy.wait()
+        sub = lax.broadcasted_iota(jnp.int32, (16, hd), 0)
+        for i in range(seqs):
+            b = c * seqs + i
+            pos = lens_ref[b] - first_pos
+            base = pl.multiple_of(lax.div(jnp.clip(pos, 0, pos_local - 1), 16) * 16, 16)
+            here = sub + base == pos
+            for which, buf in enumerate((k_buf, v_buf)):
+                old = buf[b, pl.ds(base, 16), :].astype(jnp.float32)
+                new = kv_buf[which, pl.ds(b, 1), :]
+                buf[b, pl.ds(base, 16), :] = jnp.where(here, new, old).astype(jnp.bfloat16)
+        for copy in write(c):
+            copy.start()
+        zero = jnp.zeros((16, hd), jnp.bfloat16)
+        at_pos = lax.broadcasted_iota(jnp.int32, (16, pos_local), 1) + first_pos
+        row = lax.broadcasted_iota(jnp.int32, (16, hd), 0)
+        lane = lax.broadcasted_iota(jnp.int32, (16, hd), 1)
+        pick_m = (lane == row) & (row < heads)
+        pick_l = (lane == row + 64) & (row < heads)
+        for i in range(0, seqs, 2):
+            b = c * seqs + i
+            q0 = q_buf[pl.ds(pl.multiple_of(b * 16, 16), 16), :].astype(jnp.bfloat16)
+            q1 = q_buf[pl.ds(pl.multiple_of(b * 16 + 16, 16), 16), :].astype(jnp.bfloat16)
+            q2 = jnp.concatenate([jnp.concatenate([q0, zero], axis=1), jnp.concatenate([zero, q1], axis=1)], axis=0)
+            k2 = jnp.concatenate([k_buf[b], k_buf[b + 1]], axis=1)
+            v2 = jnp.concatenate([v_buf[b], v_buf[b + 1]], axis=1)
+            s2 = lax.dot_general(q2, k2, (((1,), (1,)), ((), ())), preferred_element_type=jnp.float32) * scale
+            valid = jnp.concatenate([at_pos <= lens_ref[b], at_pos <= lens_ref[b + 1]], axis=0)
+            s2 = jnp.where(valid, s2, lowest)
+            top = jnp.max(s2, axis=-1, keepdims=True)
+            p2 = jnp.where(valid, jnp.exp(s2 - top), 0.0)
+            total = jnp.sum(p2, axis=-1, keepdims=True)
+            o2 = jnp.dot(p2.astype(jnp.bfloat16), v2, preferred_element_type=jnp.float32)
+            for e in range(2):
+                half = slice(e * 16, e * 16 + 16)
+                stat = jnp.where(pick_m, top[half], 0.0) + jnp.where(pick_l, total[half], 0.0)
+                stat = jnp.sum(stat, axis=0, keepdims=True)
+                o_buf[(i + e) * 16 : (i + e) * 16 + 16, :] = jnp.where(row == heads, stat, o2[half, e * hd : (e + 1) * hd])
+        for n in range(heads + 1):
+            part_ref[rows_of(c), n * hd : (n + 1) * hd] = o_buf[pl.ds(n, seqs, stride=16), :]
+        return 0
+
+    lax.fori_loop(0, steps, attend, 0)
+
+    def drain(c, _):
+        for copy in write(c):
+            copy.wait()
+        return 0
+
+    lax.fori_loop(0, steps, drain, 0)
+
+
+def attend(hidden, cache_lens, k_cache, v_cache, ln_gain, ln_bias, w_query, b_query, w_kv, b_kv):
+    batch, pos_local, hd = k_cache.shape
+    d_model, q_width = w_query.shape
+    heads = q_width // hd
+    blocks, steps = q_width // WIDE, batch // ATTEND_SEQS
+    f32, bf16, dma = jnp.float32, jnp.bfloat16, pltpu.SemaphoreType.DMA
+    vmem, hbm = pl.BlockSpec(memory_space=pltpu.VMEM), pl.BlockSpec(memory_space=pl.ANY)
+    return pl.pallas_call(
+        functools.partial(attend_kernel, (batch, d_model, heads, pos_local)),
+        out_shape=[
+            jax.ShapeDtypeStruct((batch, (heads + 1) * hd), f32),
+            jax.ShapeDtypeStruct(k_cache.shape, bf16),
+            jax.ShapeDtypeStruct(v_cache.shape, bf16),
+        ],
+        in_specs=[pl.BlockSpec(memory_space=pltpu.SMEM), hbm, vmem, vmem, vmem, vmem, hbm, hbm, hbm, hbm],
+        out_specs=[vmem, hbm, hbm],
+        scratch_shapes=[
+            pltpu.VMEM((batch, d_model), bf16),
+            pltpu.VMEM((W_SLOTS, d_model, WIDE), bf16),
+            pltpu.VMEM((batch * 16, hd), f32),
+            pltpu.VMEM((2, batch, hd), f32),
+            pltpu.VMEM(k_cache.shape, bf16),
+            pltpu.VMEM(v_cache.shape, bf16),
+            pltpu.VMEM((ATTEND_SEQS * 16, hd), f32),
+            dma,
+            dma((blocks + 1,)),
+            dma((2, steps)),
+            dma((2, steps)),
+        ],
+        compiler_params=pltpu.CompilerParams(vmem_limit_bytes=62 * 1024 * 1024),
+        name="attend",
+    )(
+        cache_lens,
+        hidden,
+        ln_gain.reshape(1, d_model),
+        ln_bias.reshape(1, d_model),
+        b_query.reshape(1, q_width),
+        b_kv.reshape(1, 2 * hd),
+        w_query,
+        w_kv,
+        k_cache,
+        v_cache,
+    )
+
+
 def solution(mesh):
     nx, ny = mesh.shape["sq"] // 2, mesh.shape["tp"]
 
     def local_step(hidden, cache_lens, k_cache, v_cache, ln_gain, ln_bias, w_query, b_query, w_kv, b_kv, w_out, b_out):
-        batch, pos_local, head_dim = k_cache.shape
-        heads_local = w_query.shape[1] // head_dim
-        normed = layer_norm(hidden, ln_gain, ln_bias)
-        query = (jnp.dot(normed, w_query, preferred_element_type=jnp.float32) + b_query).astype(jnp.bfloat16)
-        query = query.reshape(batch, heads_local, head_dim)
-        key_val = (jnp.dot(normed, w_kv, preferred_element_type=jnp.float32) + b_kv).astype(jnp.bfloat16)
-        first_pos = lax.axis_index("sq") * pos_local
-        positions = first_pos + lax.broadcasted_iota(jnp.int32, (1, pos_local), 1)
-        at_slot = (positions == cache_lens[:, None])[:, :, None]
-        key_new = jnp.where(at_slot, key_val[:, None, :head_dim], k_cache)
-        val_new = jnp.where(at_slot, key_val[:, None, head_dim:], v_cache)
-        scores = jnp.einsum("bnd,btd->bnt", query, key_new, preferred_element_type=jnp.float32) * (head_dim ** -0.5)
-        valid = (positions <= cache_lens[:, None])[:, None, :]
-        scores = jnp.where(valid, scores, NEG)
-        local_max = jnp.max(scores, axis=-1, keepdims=True)
-        weights = jnp.where(valid, jnp.exp(scores - local_max), 0.0)
-        local_sum = jnp.sum(weights, axis=-1)
-        numerator = jnp.einsum("bnt,btd->bnd", weights.astype(jnp.bfloat16), val_new, preferred_element_type=jnp.float32)
-        pad = ((0, 0), (0, 64 - heads_local))
-        parts = jnp.concatenate(
-            [numerator.reshape(batch, heads_local * head_dim), jnp.pad(local_max[..., 0], pad), jnp.pad(local_sum, pad)], axis=1
-        )
+        parts, key_new, val_new = attend(hidden, cache_lens, k_cache, v_cache, ln_gain, ln_bias, w_query, b_query, w_kv, b_kv)
         out_hidden = finish(parts, hidden, w_out, b_out, nx, ny)
         return out_hidden, key_new, val_new
 

time: 126 us -> 128 us (1.016)
  Pallas kernels: 54 us -> 122 us
  other arithmetic: 30.9 us -> 0 us
  matrix products: 30.1 us -> 0 us
  local copies, waits for them, and re-layouts: 9.79 us -> 4.41 us
    pallas_call x0 -> x1, Pallas kernels: none -> 68.2 us  [attend(): pl.pallas_call(functools.partial(attend_kernel, (batch, d_model, heads, p...]
    dot_general x4 -> x0, matrix products: 30.1 us -> none  [the longest x1 12.2 us: local_step(): jnp.einsum('bnd,btd->bnt', query, key_new, preferred_element_type=jnp.flo...]
    select_n x1 -> x0, other arithmetic: 23.3 us -> none  [local_step(): key_new = jnp.where(at_slot, key_val[:, None, :head_dim], k_cache)]
    reduce_sum x3 -> x0, other arithmetic: 7.43 us -> none  [the longest x1 3.9 us: local_step(): local_sum = jnp.sum(weights, axis=-1)]
    dot_general x1 -> x0, local copies, waits for them, and re-layouts: 1.63 us -> none  [local_step(): jnp.einsum('bnt,btd->bnd', weights.astype(jnp.bfloat16), val_new, preferr...]
    reshape x2 -> x1, local copies, waits for them, and re-layouts: 2.91 us -> 1.29 us  [attend(): b_query.reshape(1, q_width)]
    concatenate x1 -> x0, local copies, waits for them, and re-layouts: 1.41 us -> none  [local_step(): jnp.concatenate([numerator.reshape(batch, heads_local * head_dim), jnp.pa...]
    unnamed x23 -> x5, local copies, waits for them, and re-layouts: 3.54 us -> 3.12 us
where the time goes in v2:
time: 128 us; the launch traced here: 127 us
  Pallas kernels  122 us (95%)
  local copies, waits for them, and re-layouts  4.41 us (3%)
    pallas_call x1, Pallas kernels, attend(): pl.pallas_call(functools.partial(attend_kernel, (batch, d_model, heads, p...  68.2 us
    pallas_call x1, Pallas kernels, finish(): pl.pallas_call(functools.partial(finish_kernel, (nx, ny, heads, rows, col...  54 us
    unnamed x5, local copies, waits for them, and re-layouts  3.12 us

profile of v2, /device:TPU:97, one launch (start us, length us, event | category | flops | bytes accessed | tf_op | source)
XLA Modules:
  0.0 127.3 jit_solution(17227772004242705864)
XLA Ops:
  0.6 1.3 %reshape.23.b_query_ref = f32[1,1536]{1,0:T(1,128)} reshape(f32[1536]{0:T(1024)} %param.19) | data formatting | bytes 12288 | tf_op jit(solution)/shard_map/reshape | solution.py:473
  1.9 0.0 copy-start.1
  1.9 68.2 %attend.1 = (f32[256,1664]{1,0:T(8,128)}, bf16[256,256,128]{2,1,0:T(8,128)(2,1)}, bf16[256,256,128]{2,1,0:T(8,128)(2,1)}) custom-call(s32[256]{0:T(256)} %lens_ref.1, bf16[256,6144]{1,0:T(8,128)(2,1)} %hidden_ref.3, f32[1,6144]{1,0:T(1,128)} %bitcast.5, f32[1,6144]{1,0:T(1,128)} %bitcast.6, f32[1,1536]{1,0:T(1,128)} %reshape.23.b_query_ref, ...), custom_call_target="tpu_custom_call" | custom-call | tf_op jit(solution)/shard_map/attend/pallas_call | solution.py:444
  70.2 0.0 copy-done.1
  70.2 0.0 copy-start
  70.2 1.4 %copy-done = f32[256,1664]{1,0:T(8,128)S(1)} copy-done((f32[256,1664]{1,0:T(8,128)S(1)}, f32[256,1664]{1,0:T(8,128)}, u32[]{:S(2)}) %copy-start) | copy-done | bytes 1703960
  71.6 54.0 %finish.1 = bf16[256,6144]{1,0:T(8,128)(2,1)S(1)} custom-call(f32[256,1664]{1,0:T(8,128)S(1)} %copy-done, f32[1,6144]{1,0:T(1,128)S(1)} %bitcast.4, bf16[256,6144]{1,0:T(8,128)(2,1)} %hidden_ref.3, bf16[1536,6144]{1,0:T(8,128)(2,1)} %w_out_ref.1), custom_call_target="tpu_custom_call" | custom-call | tf_op jit(solution)/shard_map/finish/pallas_call | solution.py:248
  125.7 1.7 %copy.16 = bf16[256,6144]{1,0:T(8,128)(2,1)} copy(bf16[256,6144]{1,0:T(8,128)(2,1)S(1)} %finish.1) | data formatting | bytes 6291456
Async XLA Ops:
  1.9 68.2 %copy-start.1 = (f32[6144]{0:T(1024)S(1)}, f32[6144]{0:T(1024)}, u32[]{:S(2)}) copy-start(f32[6144]{0:T(1024)} %param.23) | copy-start | bytes 73732
  70.2 1.5 %copy-start = (f32[256,1664]{1,0:T(8,128)S(1)}, f32[256,1664]{1,0:T(8,128)}, u32[]{:S(2)}) copy-start(f32[256,1664]{1,0:T(8,128)} %get-tuple-element.6.part_ref) | copy-start | bytes 5111812

commit v3 on v2

--- a/solution.py
+++ b/solution.py
@@ -288,59 +288,16 @@
 W_SLOTS = 5
 
 
-def attend_kernel(
-    dims,
-    lens_ref,
-    hidden_ref,
-    gain_ref,
-    bias_ref,
-    b_query_ref,
-    b_kv_ref,
-    w_query_ref,
-    w_kv_ref,
-    k_ref,
-    v_ref,
-    part_ref,
-    k_out_ref,
-    v_out_ref,
-    h_buf,
-    w_buf,
-    q_buf,
-    kv_buf,
-    k_buf,
-    v_buf,
-    o_buf,
-    h_sem,
-    w_sem,
-    in_sem,
-    out_sem,
+def project_kernel(
+    dims, hidden_ref, gain_ref, bias_ref, b_query_ref, b_kv_ref, w_query_ref, w_kv_ref, q_buf, kv_buf, h_buf, w_buf, h_sem, w_sem
 ):
-    batch, d_model, heads, pos_local = dims
-    hd, seqs = LANES, ATTEND_SEQS
-    steps = batch // seqs
+    batch, d_model, heads = dims
+    hd = LANES
     blocks = heads * hd // WIDE
-    first_pos = lax.axis_index("sq") * pos_local
-    scale = hd ** -0.5
-    lowest = float(jnp.finfo(jnp.float32).min)
 
     def w_copy(k):
         src = w_kv_ref if k == 0 else w_query_ref.at[:, (k - 1) * WIDE : k * WIDE]
         return pltpu.make_async_copy(src, w_buf.at[k % W_SLOTS], w_sem.at[k])
-
-    def rows_of(c):
-        return pl.ds(pl.multiple_of(c * seqs, seqs), seqs)
-
-    def read(c):
-        return (
-            pltpu.make_async_copy(k_ref.at[rows_of(c)], k_buf.at[rows_of(c)], in_sem.at[0, c]),
-            pltpu.make_async_copy(v_ref.at[rows_of(c)], v_buf.at[rows_of(c)], in_sem.at[1, c]),
-        )
-
-    def write(c):
-        return (
-            pltpu.make_async_copy(k_buf.at[rows_of(c)], k_out_ref.at[rows_of(c)], out_sem.at[0, c]),
-            pltpu.make_async_copy(v_buf.at[rows_of(c)], v_out_ref.at[rows_of(c)], out_sem.at[1, c]),
-        )
 
     h_copy = pltpu.make_async_copy(hidden_ref, h_buf, h_sem)
     h_copy.start()
@@ -375,10 +332,49 @@
                 q_buf[pl.ds(n, batch, stride=16), :] = acc[:, e * hd : (e + 1) * hd]
         if k + W_SLOTS <= blocks:
             w_copy(k + W_SLOTS).start()
-        if k + W_SLOTS == blocks:
-            for c in range(steps):
-                for copy in read(c):
-                    copy.start()
+
+
+def attend_kernel(
+    dims,
+    lens_ref,
+    q_buf,
+    kv_buf,
+    k_ref,
+    v_ref,
+    part_ref,
+    k_out_ref,
+    v_out_ref,
+    k_buf,
+    v_buf,
+    o_buf,
+    in_sem,
+    out_sem,
+):
+    batch, d_model, heads, pos_local = dims
+    hd, seqs = LANES, ATTEND_SEQS
+    steps = batch // seqs
+    first_pos = lax.axis_index("sq") * pos_local
+    scale = hd ** -0.5
+    lowest = float(jnp.finfo(jnp.float32).min)
+
+    def rows_of(c):
+        return pl.ds(pl.multiple_of(c * seqs, seqs), seqs)
+
+    def read(c):
+        return (
+            pltpu.make_async_copy(k_ref.at[rows_of(c)], k_buf.at[rows_of(c)], in_sem.at[0, c]),
+            pltpu.make_async_copy(v_ref.at[rows_of(c)], v_buf.at[rows_of(c)], in_sem.at[1, c]),
+        )
+
+    def write(c):
+        return (
+            pltpu.make_async_copy(k_buf.at[rows_of(c)], k_out_ref.at[rows_of(c)], out_sem.at[0, c]),
+            pltpu.make_async_copy(v_buf.at[rows_of(c)], v_out_ref.at[rows_of(c)], out_sem.at[1, c]),
+        )
+
+    for c in range(steps):
+        for copy in read(c):
+            copy.start()
 
     def attend(c, _):
         for copy in read(c):
@@ -441,32 +437,20 @@
     blocks, steps = q_width // WIDE, batch // ATTEND_SEQS
     f32, bf16, dma = jnp.float32, jnp.bfloat16, pltpu.SemaphoreType.DMA
     vmem, hbm = pl.BlockSpec(memory_space=pltpu.VMEM), pl.BlockSpec(memory_space=pl.ANY)
-    return pl.pallas_call(
-        functools.partial(attend_kernel, (batch, d_model, heads, pos_local)),
-        out_shape=[
-            jax.ShapeDtypeStruct((batch, (heads + 1) * hd), f32),
-            jax.ShapeDtypeStruct(k_cache.shape, bf16),
-            jax.ShapeDtypeStruct(v_cache.shape, bf16),
-        ],
-        in_specs=[pl.BlockSpec(memory_space=pltpu.SMEM), hbm, vmem, vmem, vmem, vmem, hbm, hbm, hbm, hbm],
-        out_specs=[vmem, hbm, hbm],
+    query, key_val = pl.pallas_call(
+        functools.partial(project_kernel, (batch, d_model, heads)),
+        out_shape=[pltpu.VMEM((batch * 16, hd), f32), pltpu.VMEM((2, batch, hd), f32)],
+        in_specs=[hbm, vmem, vmem, vmem, vmem, hbm, hbm],
+        out_specs=[vmem, vmem],
         scratch_shapes=[
             pltpu.VMEM((batch, d_model), bf16),
             pltpu.VMEM((W_SLOTS, d_model, WIDE), bf16),
-            pltpu.VMEM((batch * 16, hd), f32),
-            pltpu.VMEM((2, batch, hd), f32),
-            pltpu.VMEM(k_cache.shape, bf16),
-            pltpu.VMEM(v_cache.shape, bf16),
-            pltpu.VMEM((ATTEND_SEQS * 16, hd), f32),
             dma,
             dma((blocks + 1,)),
-            dma((2, steps)),
-            dma((2, steps)),
         ],
-        compiler_params=pltpu.CompilerParams(vmem_limit_bytes=62 * 1024 * 1024),
-        name="attend",
+        compiler_params=pltpu.CompilerParams(vmem_limit_bytes=24 * 1024 * 1024),
+        name="project",
     )(
-        cache_lens,
         hidden,
         ln_gain.reshape(1, d_model),
         ln_bias.reshape(1, d_model),
@@ -474,9 +458,26 @@
         b_kv.reshape(1, 2 * hd),
         w_query,
         w_kv,
-        k_cache,
-        v_cache,
     )
+    return pl.pallas_call(
+        functools.partial(attend_kernel, (batch, d_model, heads, pos_local)),
+        out_shape=[
+            pltpu.VMEM((batch, (heads + 1) * hd), f32),
+            jax.ShapeDtypeStruct(k_cache.shape, bf16),
+            jax.ShapeDtypeStruct(v_cache.shape, bf16),
+        ],
+        in_specs=[pl.BlockSpec(memory_space=pltpu.SMEM), vmem, vmem, hbm, hbm],
+        out_specs=[vmem, hbm, hbm],
+        scratch_shapes=[
+            pltpu.VMEM(k_cache.shape, bf16),
+            pltpu.VMEM(v_cache.shape, bf16),
+            pltpu.VMEM((ATTEND_SEQS * 16, hd), f32),
+            dma((2, steps)),
+            dma((2, steps)),
+        ],
+        compiler_params=pltpu.CompilerParams(vmem_limit_bytes=40 * 1024 * 1024),
+        name="attend",
+    )(cache_lens, query, key_val, k_cache, v_cache)
 
 
 def solution(mesh):

time: 128 us -> 131 us (1.023)
  local copies, waits for them, and re-layouts: 4.41 us -> 14.7 us
  Pallas kernels: 122 us -> 115 us
    pallas_call x1, Pallas kernels: 68.2 us -> 41.9 us  [attend(): pl.pallas_call(functools.partial(attend_kernel, (batch, d_model, heads, p...]
    pallas_call x0 -> x1, Pallas kernels: none -> 19.4 us  [attend(): pl.pallas_call(functools.partial(project_kernel, (batch, d_model, heads))...]
    unnamed x5 -> x17, local copies, waits for them, and re-layouts: 3.12 us -> 14 us
where the time goes in v3:
time: 131 us
  Pallas kernels  115 us (88%)
  local copies, waits for them, and re-layouts  14.7 us (11%)
    pallas_call x1, Pallas kernels, finish(): pl.pallas_call(functools.partial(finish_kernel, (nx, ny, heads, rows, col...  54.1 us
    pallas_call x1, Pallas kernels, attend(): pl.pallas_call(functools.partial(attend_kernel, (batch, d_model, heads, p...  41.9 us
    pallas_call x1, Pallas kernels, attend(): pl.pallas_call(functools.partial(project_kernel, (batch, d_model, heads))...  19.4 us
    unnamed x17, local copies, waits for them, and re-layouts  14 us

profile of v3, /device:TPU:97, one launch (start us, length us, event | category | flops | bytes accessed | tf_op | source)
XLA Modules:
  0.0 130.8 jit_solution(10480918262984485974)
XLA Ops:
  0.6 0.0 copy-start.7
  0.6 0.7 reshape.23.b_query_ref
  1.3 0.0 copy-start
  1.4 6.4 %copy-done = bf16[6144,1536]{1,0:T(8,128)(2,1)S(1)} copy-done((bf16[6144,1536]{1,0:T(8,128)(2,1)S(1)}, bf16[6144,1536]{1,0:T(8,128)(2,1)}, u32[]{:S(2)}) %copy-start) | copy-done | bytes 18874392
  7.7 0.0 copy-start.1
  7.7 1.9 %copy-done.1 = bf16[256,6144]{1,0:T(8,128)(2,1)S(1)} copy-done((bf16[256,6144]{1,0:T(8,128)(2,1)S(1)}, bf16[256,6144]{1,0:T(8,128)(2,1)}, u32[]{:S(2)}) %copy-start.1) | copy-done | bytes 3145752
  9.6 0.0 copy-start.2
  9.6 1.9 %copy-done.2 = bf16[6144,256]{1,0:T(8,128)(2,1)S(1)} copy-done((bf16[6144,256]{1,0:T(8,128)(2,1)S(1)}, bf16[6144,256]{1,0:T(8,128)(2,1)}, u32[]{:S(2)}) %copy-start.2) | copy-done | bytes 3145752
  11.5 0.0 copy-start.3
  11.5 0.7 copy-done.3
  12.2 0.0 copy-start.4
  12.2 0.7 copy-done.4
  13.0 0.0 copy-start.6
  13.0 0.7 copy-done.6
  13.7 19.4 %project.1 = (f32[4096,128]{1,0:T(8,128)S(1)}, f32[2,256,128]{2,1,0:T(8,128)S(1)}) custom-call(bf16[256,6144]{1,0:T(8,128)(2,1)S(1)} %copy-done.1, f32[1,6144]{1,0:T(1,128)S(1)} %bitcast.4, f32[1,6144]{1,0:T(1,128)S(1)} %bitcast.5, f32[1,1536]{1,0:T(1,128)S(1)} %reshape.23.b_query_ref, f32[1,256]{1,0:T(1,128)S(1)} %bitcast.7, ...), custom_call_target="tpu_custom_call" | custom-call | tf_op jit(solution)/shard_map/project/pallas_call | solution.py:440
  33.1 0.0 copy-done.7
  33.1 0.0 copy-start.5
  33.1 41.9 %attend.1 = (f32[256,1664]{1,0:T(8,128)S(1)}, bf16[256,256,128]{2,1,0:T(8,128)(2,1)}, bf16[256,256,128]{2,1,0:T(8,128)(2,1)}) custom-call(s32[256]{0:T(256)S(1)} %copy-done.7, f32[4096,128]{1,0:T(8,128)S(1)} %get-tuple-element.8.q_buf, f32[2,256,128]{2,1,0:T(8,128)S(1)} %get-tuple-element.9.kv_buf, bf16[256,256,128]{2,1,0:T(8,128)(2,1)} %k_ref.1, ...), custom_call_target="tpu_custom_call" | custom-call | tf_op jit(solution)/shard_map/attend/pallas_call | solution.py:462
  75.0 0.0 copy-done.5
  75.0 54.1 %finish.1 = bf16[256,6144]{1,0:T(8,128)(2,1)S(1)} custom-call(f32[256,1664]{1,0:T(8,128)S(1)} %get-tuple-element.10.part_ref, f32[1,6144]{1,0:T(1,128)S(1)} %bitcast.6, bf16[256,6144]{1,0:T(8,128)(2,1)} %hidden_ref.3, bf16[1536,6144]{1,0:T(8,128)(2,1)} %w_out_ref.1), custom_call_target="tpu_custom_call" | custom-call | tf_op jit(solution)/shard_map/finish/pallas_call | solution.py:248
  129.1 1.7 %copy.16 = bf16[256,6144]{1,0:T(8,128)(2,1)} copy(bf16[256,6144]{1,0:T(8,128)(2,1)S(1)} %finish.1) | data formatting | bytes 6291456
Async XLA Ops:
  0.6 32.4 %copy-start.7 = (s32[256]{0:T(256)S(1)}, s32[256]{0:T(256)}, u32[]{:S(2)}) copy-start(s32[256]{0:T(256)} %lens_ref.1) | copy-start | bytes 3076
  1.3 6.4 %copy-start = (bf16[6144,1536]{1,0:T(8,128)(2,1)S(1)}, bf16[6144,1536]{1,0:T(8,128)(2,1)}, u32[]{:S(2)}) copy-start(bf16[6144,1536]{1,0:T(8,128)(2,1)} %w_query_ref.1) | copy-start | bytes 56623108
  7.7 1.9 %copy-start.1 = (bf16[256,6144]{1,0:T(8,128)(2,1)S(1)}, bf16[256,6144]{1,0:T(8,128)(2,1)}, u32[]{:S(2)}) copy-start(bf16[256,6144]{1,0:T(8,128)(2,1)} %hidden_ref.3) | copy-start | bytes 9437188
  9.6 1.9 %copy-start.2 = (bf16[6144,256]{1,0:T(8,128)(2,1)S(1)}, bf16[6144,256]{1,0:T(8,128)(2,1)}, u32[]{:S(2)}) copy-start(bf16[6144,256]{1,0:T(8,128)(2,1)} %w_kv_ref.1) | copy-start | bytes 9437188
  11.5 0.7 copy-start.3
  12.2 0.7 copy-start.4
  13.0 0.7 copy-start.6
  33.1 41.9 %copy-start.5 = (f32[6144]{0:T(1024)S(1)}, f32[6144]{0:T(1024)}, u32[]{:S(2)}) copy-start(f32[6144]{0:T(1024)} %param.23) | copy-start | bytes 73732

commit v4 on v2

--- a/solution.py
+++ b/solution.py
@@ -310,6 +310,10 @@
     k_buf,
     v_buf,
     o_buf,
+    s_buf0,
+    s_buf1,
+    stat_buf,
+    stat_buf2,
     h_sem,
     w_sem,
     in_sem,
@@ -349,16 +353,44 @@
     q_buf[...] = jnp.zeros_like(q_buf)
     h_copy.wait()
 
+    tiles = d_model // hd
+
+    def lane_tiles(at):
+        return [h_buf[at, t * hd : (t + 1) * hd].astype(jnp.float32) for t in range(tiles)]
+
+    def add_up(values):
+        while len(values) > 1:
+            values = [sum(values[i : i + 2]) for i in range(0, len(values), 2)]
+        return values[0]
+
+    def rows16(r):
+        return pl.ds(pl.multiple_of(r * 16, 16), 16)
+
+    def sum_rows(r, _):
+        stat_buf[rows16(r), :] = add_up(lane_tiles(rows16(r)))
+        return 0
+
+    def spread_rows(r, _):
+        mean_val = stat_buf[rows16(r), :]
+        stat_buf2[rows16(r), :] = add_up([(v - mean_val) * (v - mean_val) for v in lane_tiles(rows16(r))])
+        return 0
+
     def norm_rows(r, _):
-        at = pl.ds(pl.multiple_of(r * 16, 16), 16)
-        x_wide = h_buf[at, :].astype(jnp.float32)
-        mean_val = jnp.sum(x_wide, axis=-1, keepdims=True) * (1.0 / d_model)
-        centered = x_wide - mean_val
-        variance = jnp.sum(centered * centered, axis=-1, keepdims=True) * (1.0 / d_model)
-        normed = centered * lax.rsqrt(variance + 1e-5)
-        h_buf[at, :] = (normed * gain_ref[...] + bias_ref[...]).astype(jnp.bfloat16)
+        at = rows16(r)
+        mean_val, inv = stat_buf[at, :], stat_buf2[at, :]
+        for t in range(tiles):
+            cols = slice(t * hd, (t + 1) * hd)
+            normed = (h_buf[at, cols].astype(jnp.float32) - mean_val) * inv
+            h_buf[at, cols] = (normed * gain_ref[:, cols] + bias_ref[:, cols]).astype(jnp.bfloat16)
         return 0
 
+    def row_means(buf):
+        return jnp.broadcast_to(jnp.sum(buf[...], axis=-1, keepdims=True) * (1.0 / d_model), buf.shape)
+
+    lax.fori_loop(0, batch // 16, sum_rows, 0)
+    stat_buf[...] = row_means(stat_buf)
+    lax.fori_loop(0, batch // 16, spread_rows, 0)
+    stat_buf2[...] = lax.rsqrt(row_means(stat_buf2) + 1e-5)
     lax.fori_loop(0, batch // 16, norm_rows, 0)
 
     for k in range(blocks + 1):
@@ -380,37 +412,44 @@
                 for copy in read(c):
                     copy.start()
 
-    def attend(c, _):
+    zero = jnp.zeros((16, hd), jnp.bfloat16)
+    at_pos = lax.broadcasted_iota(jnp.int32, (16, pos_local), 1) + first_pos
+    row = lax.broadcasted_iota(jnp.int32, (16, hd), 0)
+    lane = lax.broadcasted_iota(jnp.int32, (16, hd), 1)
+    pick_m = (lane == row) & (row < heads)
+    pick_l = (lane == row + 64) & (row < heads)
+
+    def take(c):
         for copy in read(c):
             copy.wait()
-        sub = lax.broadcasted_iota(jnp.int32, (16, hd), 0)
         for i in range(seqs):
             b = c * seqs + i
             pos = lens_ref[b] - first_pos
             base = pl.multiple_of(lax.div(jnp.clip(pos, 0, pos_local - 1), 16) * 16, 16)
-            here = sub + base == pos
+            here = row + base == pos
             for which, buf in enumerate((k_buf, v_buf)):
                 old = buf[b, pl.ds(base, 16), :].astype(jnp.float32)
                 new = kv_buf[which, pl.ds(b, 1), :]
                 buf[b, pl.ds(base, 16), :] = jnp.where(here, new, old).astype(jnp.bfloat16)
         for copy in write(c):
             copy.start()
-        zero = jnp.zeros((16, hd), jnp.bfloat16)
-        at_pos = lax.broadcasted_iota(jnp.int32, (16, pos_local), 1) + first_pos
-        row = lax.broadcasted_iota(jnp.int32, (16, hd), 0)
-        lane = lax.broadcasted_iota(jnp.int32, (16, hd), 1)
-        pick_m = (lane == row) & (row < heads)
-        pick_l = (lane == row + 64) & (row < heads)
+
+    def score(c, s_buf):
         for i in range(0, seqs, 2):
             b = c * seqs + i
             q0 = q_buf[pl.ds(pl.multiple_of(b * 16, 16), 16), :].astype(jnp.bfloat16)
             q1 = q_buf[pl.ds(pl.multiple_of(b * 16 + 16, 16), 16), :].astype(jnp.bfloat16)
             q2 = jnp.concatenate([jnp.concatenate([q0, zero], axis=1), jnp.concatenate([zero, q1], axis=1)], axis=0)
             k2 = jnp.concatenate([k_buf[b], k_buf[b + 1]], axis=1)
+            s2 = lax.dot_general(q2, k2, (((1,), (1,)), ((), ())), preferred_element_type=jnp.float32)
+            s_buf[i * 16 : i * 16 + 32, :] = s2 * scale
+
+    def combine(c, s_buf):
+        for i in range(0, seqs, 2):
+            b = c * seqs + i
             v2 = jnp.concatenate([v_buf[b], v_buf[b + 1]], axis=1)
-            s2 = lax.dot_general(q2, k2, (((1,), (1,)), ((), ())), preferred_element_type=jnp.float32) * scale
             valid = jnp.concatenate([at_pos <= lens_ref[b], at_pos <= lens_ref[b + 1]], axis=0)
-            s2 = jnp.where(valid, s2, lowest)
+            s2 = jnp.where(valid, s_buf[i * 16 : i * 16 + 32, :], lowest)
             top = jnp.max(s2, axis=-1, keepdims=True)
             p2 = jnp.where(valid, jnp.exp(s2 - top), 0.0)
             total = jnp.sum(p2, axis=-1, keepdims=True)
@@ -422,9 +461,25 @@
                 o_buf[(i + e) * 16 : (i + e) * 16 + 16, :] = jnp.where(row == heads, stat, o2[half, e * hd : (e + 1) * hd])
         for n in range(heads + 1):
             part_ref[rows_of(c), n * hd : (n + 1) * hd] = o_buf[pl.ds(n, seqs, stride=16), :]
+
+    take(0)
+    score(0, s_buf0)
+
+    def two_steps(t, _):
+        c = t * 2
+        take(c + 1)
+        score(c + 1, s_buf1)
+        combine(c, s_buf0)
+        take(c + 2)
+        score(c + 2, s_buf0)
+        combine(c + 1, s_buf1)
         return 0
 
-    lax.fori_loop(0, steps, attend, 0)
+    lax.fori_loop(0, steps // 2 - 1, two_steps, 0)
+    take(steps - 1)
+    score(steps - 1, s_buf1)
+    combine(steps - 2, s_buf0)
+    combine(steps - 1, s_buf1)
 
     def drain(c, _):
         for copy in write(c):
@@ -444,7 +499,7 @@
     return pl.pallas_call(
         functools.partial(attend_kernel, (batch, d_model, heads, pos_local)),
         out_shape=[
-            jax.ShapeDtypeStruct((batch, (heads + 1) * hd), f32),
+            pltpu.VMEM((batch, (heads + 1) * hd), f32),
             jax.ShapeDtypeStruct(k_cache.shape, bf16),
             jax.ShapeDtypeStruct(v_cache.shape, bf16),
         ],
@@ -458,12 +513,16 @@
             pltpu.VMEM(k_cache.shape, bf16),
             pltpu.VMEM(v_cache.shape, bf16),
             pltpu.VMEM((ATTEND_SEQS * 16, hd), f32),
+            pltpu.VMEM((ATTEND_SEQS * 16, pos_local), f32),
+            pltpu.VMEM((ATTEND_SEQS * 16, pos_local), f32),
+            pltpu.VMEM((batch, hd), f32),
+            pltpu.VMEM((batch, hd), f32),
             dma,
             dma((blocks + 1,)),
             dma((2, steps)),
             dma((2, steps)),
         ],
-        compiler_params=pltpu.CompilerParams(vmem_limit_bytes=62 * 1024 * 1024),
+        compiler_params=pltpu.CompilerParams(vmem_limit_bytes=60 * 1024 * 1024),
         name="attend",
     )(
         cache_lens,

time: 128 us -> 96.2 us (0.75)
  Pallas kernels: 122 us -> 92.4 us
  local copies, waits for them, and re-layouts: 4.41 us -> 2.97 us
    pallas_call x1, Pallas kernels: 68.2 us -> 38.3 us  [attend(): pl.pallas_call(functools.partial(attend_kernel, (batch, d_model, heads, p...]
    unnamed x5 -> x3, local copies, waits for them, and re-layouts: 3.12 us -> 1.67 us
where the time goes in v4:
time: 96.2 us; the launch traced here: 96 us
  Pallas kernels  92.4 us (96%)
  local copies, waits for them, and re-layouts  2.97 us (3%)
    pallas_call x1, Pallas kernels, finish(): pl.pallas_call(functools.partial(finish_kernel, (nx, ny, heads, rows, col...  54.1 us
    pallas_call x1, Pallas kernels, attend(): pl.pallas_call(functools.partial(attend_kernel, (batch, d_model, heads, p...  38.3 us

profile of v4, /device:TPU:97, one launch (start us, length us, event | category | flops | bytes accessed | tf_op | source)
XLA Modules:
  0.0 96.0 jit_solution(1372932736650286184)
XLA Ops:
  0.6 1.3 %reshape.23.b_query_ref = f32[1,1536]{1,0:T(1,128)} reshape(f32[1536]{0:T(1024)} %param.19) | data formatting | bytes 12288 | tf_op jit(solution)/shard_map/reshape | solution.py:532
  1.9 0.0 copy-start
  1.9 38.3 %attend.1 = (f32[256,1664]{1,0:T(8,128)S(1)}, bf16[256,256,128]{2,1,0:T(8,128)(2,1)}, bf16[256,256,128]{2,1,0:T(8,128)(2,1)}) custom-call(s32[256]{0:T(256)} %lens_ref.1, bf16[256,6144]{1,0:T(8,128)(2,1)} %hidden_ref.3, f32[1,6144]{1,0:T(1,128)} %bitcast.5, f32[1,6144]{1,0:T(1,128)} %bitcast.6, f32[1,1536]{1,0:T(1,128)} %reshape.23.b_query_ref, ...), custom_call_target="tpu_custom_call" | custom-call | tf_op jit(solution)/shard_map/attend/pallas_call | solution.py:499
  40.2 0.0 copy-done
  40.2 54.1 %finish.1 = bf16[256,6144]{1,0:T(8,128)(2,1)S(1)} custom-call(f32[256,1664]{1,0:T(8,128)S(1)} %get-tuple-element.6.part_ref, f32[1,6144]{1,0:T(1,128)S(1)} %bitcast.4, bf16[256,6144]{1,0:T(8,128)(2,1)} %hidden_ref.3, bf16[1536,6144]{1,0:T(8,128)(2,1)} %w_out_ref.1), custom_call_target="tpu_custom_call" | custom-call | tf_op jit(solution)/shard_map/finish/pallas_call | solution.py:248
  94.4 1.7 %copy.16 = bf16[256,6144]{1,0:T(8,128)(2,1)} copy(bf16[256,6144]{1,0:T(8,128)(2,1)S(1)} %finish.1) | data formatting | bytes 6291456
Async XLA Ops:
  1.9 38.3 %copy-start = (f32[6144]{0:T(1024)S(1)}, f32[6144]{0:T(1024)}, u32[]{:S(2)}) copy-start(f32[6144]{0:T(1024)} %param.23) | copy-start | bytes 73732

commit v5 on v1

v5 whole, which is shorter than its diff:
```python
import functools

import jax
import jax.numpy as jnp
from jax import lax
from jax.experimental import pallas as pl
from jax.experimental.pallas import tpu as pltpu
from jax.sharding import PartitionSpec as P

MESH = pl.DeviceIdType.MESH
LANES = 128
SEQS = 16
WIDE = 256
W_SLOTS = 3


def merge_into(dst, part_a, part_b, heads):
    stat_a, stat_b = part_a(heads), part_b(heads)
    top = jnp.maximum(stat_a, stat_b)
    exp_a, exp_b = jnp.exp(stat_a - top), jnp.exp(stat_b - top)
    sums = stat_a * pltpu.roll(exp_a, 64, 1) + stat_b * pltpu.roll(exp_b, 64, 1)
    lane = lax.broadcasted_iota(jnp.int32, top.shape, 1)
    stat = jnp.where(lane < 64, top, sums)
    for n in range(heads):
        dst[:, n * LANES : (n + 1) * LANES] = part_a(n) * exp_a[:, n : n + 1] + part_b(n) * exp_b[:, n : n + 1]
    dst[:, heads * LANES :] = stat


def decode_kernel(
    dims,
    lens_ref,
    gain_ref,
    bias_ref,
    b_query_ref,
    b_kv_ref,
    b_out_ref,
    hidden_ref,
    w_query_ref,
    w_kv_ref,
    w_out_ref,
    k_ref,
    v_ref,
    out_ref,
    kv_buf,
    cache_buf,
    w_buf,
    q_buf,
    part_buf,
    o_buf,
    s_buf0,
    s_buf1,
    stat_buf,
    stat_buf2,
    pair_buf,
    x_buf,
    att_buf,
    proj_buf,
    y_buf,
    hid_buf,
    gather_buf,
    h_sem,
    w_sem,
    in_sem,
    wo_sem,
    hid_sem,
    pair_send,
    pair_recv,
    x_send,
    x_recv,
    y_send,
    y_recv,
    g_send,
    g_recv,
    d_send,
    d_recv,
):
    nx, ny, heads, rows, cols, pos_local = dims
    k_buf, v_buf = cache_buf.at[0], cache_buf.at[1]
    batch, d_model = out_ref.shape
    hd, seqs = LANES, SEQS
    half = cols // 2
    depth = heads * hd
    steps = batch // seqs
    blocks = depth // WIDE
    sq = lax.axis_index("sq")
    y = lax.axis_index("tp")
    x = sq // 2
    core = sq % 2
    step = 1 - 2 * core
    first_pos = sq * pos_local
    scale = hd ** -0.5
    lowest = float(jnp.finfo(jnp.float32).min)

    def wrap(value, size):
        return lax.rem(value + 2 * size, size)

    x_fwd, x_bwd, x_opp = wrap(x + step, nx), wrap(x - step, nx), wrap(x + 2, nx)
    y_fwd, y_bwd, y_opp = wrap(y + step, ny), wrap(y - step, ny), wrap(y + 2, ny)
    to_pair = {"sq": x * 2 + 1 - core}
    to_x_fwd, to_x_bwd = {"sq": x_fwd * 2 + core}, {"sq": x_bwd * 2 + core}
    to_y_fwd, to_y_bwd = {"tp": y_fwd}, {"tp": y_bwd}

    barrier = pltpu.get_barrier_semaphore()
    for peer in (to_pair, to_x_fwd, to_x_bwd, to_y_fwd, to_y_bwd):
        pl.semaphore_signal(barrier, inc=1, device_id=peer, device_id_type=MESH)

    h_buf = out_ref

    def w_copy(k):
        src = w_kv_ref if k == 0 else w_query_ref.at[:, (k - 1) * WIDE : k * WIDE]
        return pltpu.make_async_copy(src, w_buf.at[k % W_SLOTS], w_sem.at[k])

    def block_row(i):
        slot, mine = i // 2, i % 2
        sign = step * (1 - 2 * mine)
        shift = 2 * ((3 - slot) // 3) + sign * (slot * (3 - slot) * (3 - 2 * slot) // 2)
        owner = wrap(x + shift, nx) * 2 + (1 - core) * (1 - mine) + core * mine
        return owner * rows

    def step_rows(c):
        per = rows // seqs
        return pl.multiple_of(block_row(c // per) + (c % per) * seqs, seqs)

    def read(c):
        at = pl.ds(step_rows(c), seqs)
        return (
            pltpu.make_async_copy(k_ref.at[at], k_buf.at[at], in_sem.at[0, c]),
            pltpu.make_async_copy(v_ref.at[at], v_buf.at[at], in_sem.at[1, c]),
        )

    h_copy = pltpu.make_async_copy(hidden_ref, h_buf, h_sem)
    h_copy.start()
    for k in range(W_SLOTS):
        w_copy(k).start()
    q_buf[...] = jnp.zeros_like(q_buf)
    h_copy.wait()

    tiles = d_model // hd

    def lane_tiles(at):
        return [h_buf[at, t * hd : (t + 1) * hd].astype(jnp.float32) for t in range(tiles)]

    def add_up(values):
        while len(values) > 1:
            values = [sum(values[i : i + 2]) for i in range(0, len(values), 2)]
        return values[0]

    def rows16(r):
        return pl.ds(pl.multiple_of(r * 16, 16), 16)

    def sum_rows(r, _):
        stat_buf[rows16(r), :] = add_up(lane_tiles(rows16(r)))
        return 0

    def spread_rows(r, _):
        mean_val = stat_buf[rows16(r), :]
        stat_buf2[rows16(r), :] = add_up([(v - mean_val) * (v - mean_val) for v in lane_tiles(rows16(r))])
        return 0

    def norm_rows(r, _):
        at = rows16(r)
        mean_val, inv = stat_buf[at, :], stat_buf2[at, :]
        for t in range(tiles):
            cols = slice(t * hd, (t + 1) * hd)
            normed = (h_buf[at, cols].astype(jnp.float32) - mean_val) * inv
            h_buf[at, cols] = (normed * gain_ref[:, cols] + bias_ref[:, cols]).astype(jnp.bfloat16)
        return 0

    def row_means(buf):
        return jnp.broadcast_to(jnp.sum(buf[...], axis=-1, keepdims=True) * (1.0 / d_model), buf.shape)

    lax.fori_loop(0, batch // 16, sum_rows, 0)
    stat_buf[...] = row_means(stat_buf)
    lax.fori_loop(0, batch // 16, spread_rows, 0)
    stat_buf2[...] = lax.rsqrt(row_means(stat_buf2) + 1e-5)
    lax.fori_loop(0, batch // 16, norm_rows, 0)

    units = ((0, 0), (0, 1), (1, 0), (2, 0), (3, 0), (1, 1), (2, 1), (3, 1))
    y_order = (y_opp, y_bwd, y_fwd, y)
    per_unit, per_slot = half // WIDE, d_model // depth

    def wo_place(u, j):
        at = (u % 4) * per_unit + j
        return at // per_slot, slice((at % per_slot) * depth, (at % per_slot + 1) * depth)

    def wo_copies(u):
        target, h = units[u]
        copies = []
        for j in range(per_unit):
            col = pl.multiple_of(y_order[target] * cols + h * half + j * WIDE, WIDE)
            slot, at = wo_place(u, j)
            copies.append(
                pltpu.make_async_copy(w_out_ref.at[:, pl.ds(col, WIDE)], w_buf.at[slot, at, :], wo_sem.at[u, j])
            )
        return copies

    for k in range(blocks + 1):
        w_copy(k).wait()
        acc = jnp.dot(h_buf[...], w_buf[k % W_SLOTS], preferred_element_type=jnp.float32)
        if k == 0:
            acc = (acc + b_kv_ref[...]).astype(jnp.bfloat16).astype(jnp.float32)
            kv_buf[0] = acc[:, :hd]
            kv_buf[1] = acc[:, hd:]
        else:
            bias = b_query_ref[(k - 1) * WIDE : k * WIDE].reshape(1, WIDE)
            acc = (acc + bias).astype(jnp.bfloat16).astype(jnp.float32)
            for e in range(WIDE // hd):
                n = (k - 1) * (WIDE // hd) + e
                q_buf[pl.ds(n, batch, stride=16), :] = acc[:, e * hd : (e + 1) * hd]
        if k + W_SLOTS <= blocks:
            w_copy(k + W_SLOTS).start()
        if k + W_SLOTS == blocks:
            for c in range(steps):
                for copy in read(c):
                    copy.start()
    hid_copy = pltpu.make_async_copy(
        hidden_ref.at[pl.ds(pl.multiple_of(sq * rows, rows), rows), pl.ds(pl.multiple_of(y * cols, cols), cols)], hid_buf, hid_sem
    )
    hid_copy.start()
    for u in range(4):
        for copy in wo_copies(u):
            copy.start()

    zero = jnp.zeros((16, hd), jnp.bfloat16)
    at_pos = lax.broadcasted_iota(jnp.int32, (16, pos_local), 1) + first_pos
    row = lax.broadcasted_iota(jnp.int32, (16, hd), 0)
    lane = lax.broadcasted_iota(jnp.int32, (16, hd), 1)
    pick_m = (lane == row) & (row < heads)
    pick_l = (lane == row + 64) & (row < heads)

    def score(c, s_buf):
        for copy in read(c):
            copy.wait()
        b0 = step_rows(c)
        for i in range(0, seqs, 2):
            q0 = q_buf[pl.ds(pl.multiple_of(b0 * 16 + i * 16, 16), 16), :].astype(jnp.bfloat16)
            q1 = q_buf[pl.ds(pl.multiple_of(b0 * 16 + i * 16 + 16, 16), 16), :].astype(jnp.bfloat16)
            q2 = jnp.concatenate([jnp.concatenate([q0, zero], axis=1), jnp.concatenate([zero, q1], axis=1)], axis=0)
            k2 = jnp.concatenate([k_buf[b0 + i], k_buf[b0 + i + 1]], axis=1)
            s2 = lax.dot_general(q2, k2, (((1,), (1,)), ((), ())), preferred_element_type=jnp.float32)
            s_buf[i * 16 : i * 16 + 32, :] = s2 * scale

    def combine(c, s_buf):
        b0 = step_rows(c)
        for i in range(0, seqs, 2):
            v2 = jnp.concatenate([v_buf[b0 + i], v_buf[b0 + i + 1]], axis=1)
            valid = jnp.concatenate([at_pos < lens_ref[b0 + i], at_pos < lens_ref[b0 + i + 1]], axis=0)
            s2 = jnp.where(valid, s_buf[i * 16 : i * 16 + 32, :], lowest)
            top = jnp.max(s2, axis=-1, keepdims=True)
            p2 = jnp.where(valid, jnp.exp(s2 - top), 0.0)
            total = jnp.sum(p2, axis=-1, keepdims=True)
            o2 = jnp.dot(p2.astype(jnp.bfloat16), v2, preferred_element_type=jnp.float32)
            for e in range(2):
                part = slice(e * 16, e * 16 + 16)
                stat = jnp.where(pick_m, top[part], 0.0) + jnp.where(pick_l, total[part], 0.0)
                stat = jnp.sum(stat, axis=0, keepdims=True)
                o_buf[(i + e) * 16 : (i + e) * 16 + 16, :] = jnp.where(row == heads, stat, o2[part, e * hd : (e + 1) * hd])
        for n in range(heads + 1):
            part_buf[pl.ds(b0, seqs), n * hd : (n + 1) * hd] = o_buf[pl.ds(n, seqs, stride=16), :]

    sends = []

    def remote(src, dst, ssem, rsem, peer):
        return pltpu.make_async_remote_copy(
            src_ref=src, dst_ref=dst, send_sem=ssem, recv_sem=rsem, device_id=peer, device_id_type=MESH
        )

    def send(*args):
        copy = remote(*args)
        copy.start()
        sends.append(copy)
        return copy

    def part_at(i):
        return pl.ds(pl.multiple_of(block_row(i), rows), rows)

    def of_part(i):
        return lambda n: part_buf[part_at(i), n * hd : (n + 1) * hd]

    def of(ref):
        return lambda n: ref[:, n * hd : (n + 1) * hd]

    pair = [remote(part_buf.at[part_at(2 * k), :], pair_buf.at[k], pair_send.at[k], pair_recv.at[k], to_pair) for k in range(4)]
    x_o = remote(pair_buf.at[0], x_buf.at[0], x_send.at[0], x_recv.at[0], to_x_fwd)
    x_b = remote(pair_buf.at[1], x_buf.at[1], x_send.at[1], x_recv.at[1], to_x_bwd)
    x_a = remote(pair_buf.at[2], x_buf.at[2], x_send.at[2], x_recv.at[2], to_x_fwd)
    sends.extend(pair + [x_o, x_b, x_a])

    def after_block(i):
        slot = i // 2
        if i % 2 == 0:
            pair[slot].start()
            return
        pair[slot].wait_recv()
        merge_into(pair_buf.at[slot], of_part(i), of(pair_buf.at[slot]), heads)
        if slot == 0:
            x_o.start()
        elif slot == 1:
            x_b.start()
        elif slot == 2:
            x_o.wait_recv()
            merge_into(pair_buf.at[2], of(pair_buf.at[2]), of(x_buf.at[0]), heads)
            x_a.start()

    pl.semaphore_wait(barrier, 5)
    score(0, s_buf0)

    def one_block(i, _):
        c = i * 2
        score(c + 1, s_buf1)
        combine(c, s_buf0)
        score(c + 2, s_buf0)
        combine(c + 1, s_buf1)
        for j in range(7):
            pl.when(i == j)(functools.partial(after_block, j))
        return 0

    lax.fori_loop(0, steps // 2 - 1, one_block, 0)
    score(steps - 1, s_buf1)
    combine(steps - 2, s_buf0)
    combine(steps - 1, s_buf1)

    own = pl.multiple_of(sq * rows, rows)
    k_new, v_new = kv_buf[0, pl.ds(own, rows), :], kv_buf[1, pl.ds(own, rows), :]
    new_lane = lax.broadcasted_iota(jnp.int32, (rows, hd), 1)
    new_stat = jnp.where((new_lane >= 64) & (new_lane < 64 + heads), 1.0, 0.0)
    for n in range(heads):
        s_new = jnp.sum(q_buf[pl.ds(own * 16 + n, rows, stride=16), :] * k_new, axis=-1, keepdims=True) * scale
        new_stat = jnp.where(new_lane == n, s_new, new_stat)

    after_block(7)
    total = pair_buf.at[3]
    merge_into(total, of(total), lambda n: new_stat if n == heads else v_new, heads)
    x_b.wait_recv()
    merge_into(total, of(total), of(x_buf.at[1]), heads)
    x_a.wait_recv()
    merge_into(total, of(total), of(x_buf.at[2]), heads)
    stat = total[:, depth:]
    for n in range(heads):
        block = slice(n * hd, (n + 1) * hd)
        att_buf[:, block] = (total[:, block] / stat[:, 64 + n : 65 + n]).astype(jnp.bfloat16)

    def project(u):
        for copy in wo_copies(u):
            copy.wait()
        parts = []
        for j in range(per_unit):
            slot, at = wo_place(u, j)
            parts.append(jnp.dot(att_buf[...], w_buf[slot, at, :], preferred_element_type=jnp.float32))
        return jnp.concatenate(parts, axis=1)

    def refill(u):
        if u + 4 < len(units):
            for copy in wo_copies(u + 4):
                copy.start()

    y_o, y_b, y_a = [None, None], [None, None], [None, None]
    for u, (target, h) in enumerate(units):
        if target < 2:
            proj_buf[target, h] = project(u)
            refill(u)
            peer = (to_y_fwd, to_y_bwd)[target]
            copy = send(proj_buf.at[target, h], y_buf.at[target, h], y_send.at[target, h], y_recv.at[target, h], peer)
            (y_o, y_b)[target][h] = copy
        elif target == 2:
            fwd_part = project(u)
            refill(u)
            y_o[h].wait_recv()
            proj_buf[2, h] = fwd_part + y_buf[0, h]
            y_a[h] = send(proj_buf.at[2, h], y_buf.at[2, h], y_send.at[2, h], y_recv.at[2, h], to_y_fwd)
        else:
            if h == 0:
                hid_copy.wait()
            own_cols = pl.ds(pl.multiple_of(y * cols + h * half, half), half)
            proj_buf[3, h] = project(u) + hid_buf[:, h * half : (h + 1) * half].astype(jnp.float32) + b_out_ref[:, own_cols]
            refill(u)

    def place(xt, yt, ct, h):
        row = pl.multiple_of((xt * 2 + ct) * rows, rows)
        col = pl.multiple_of(yt * cols + h * half, half)
        return pl.ds(row, rows), pl.ds(col, half)

    xs = (x, x_bwd, x_fwd, x_opp)
    ys = (y, y_bwd, y_fwd, y_opp)
    x_peers, y_peers = (to_x_fwd, to_x_bwd), (to_y_fwd, to_y_bwd)
    gathers = {}
    pairs = {}

    def spot(h, first, second, ct=None):
        ct = core if ct is None else ct
        if h == 0:
            return place(xs[first], ys[second], ct, h)
        return place(xs[second], ys[first], ct, h)

    def piece(h, first, second):
        return gather_buf.at[spot(h, first, second)]

    def ring_send(h, first, second, slot, phase):
        peers = (x_peers, y_peers) if h == 0 else (y_peers, x_peers)
        peer = peers[phase][1 if slot == 2 else 0]
        index = slot - 1 if phase == 0 else 3 + first * 3 + slot - 1
        key = (h, phase, first if phase else 0, slot)
        ref = piece(h, first, second)
        gathers[key] = send(ref, ref, g_send.at[h, index], g_recv.at[h, index], peer)

    def pair_forward(h, first, second):
        ref = piece(h, first, second)
        index = first * 4 + second
        pairs[(h, first, second)] = send(ref, ref, d_send.at[h, index], d_recv.at[h, index], to_pair)

    def convert(where):
        out_ref[where] = gather_buf[where].astype(jnp.bfloat16)

    def mirrored(slot):
        return (0, 2, 1, 3)[slot]

    todo = []

    def drain(limit):
        while len(todo) > limit:
            h, first, second = todo.pop(0)
            pairs[(h, first, second)].wait_recv()
            convert(spot(h, mirrored(first), mirrored(second), 1 - core))

    def have(h, first, second):
        pair_forward(h, first, second)
        convert(spot(h, first, second))
        todo.append((h, first, second))
        drain(2)

    for h in range(2):
        y_b[h].wait_recv()
        part = proj_buf[3, h] + y_buf[1, h]
        y_a[h].wait_recv()
        gather_buf[spot(h, 0, 0)] = part + y_buf[2, h]
        ring_send(h, 0, 0, 1, 0)
        ring_send(h, 0, 0, 2, 0)
        pair_forward(h, 0, 0)
    for h in range(2):
        ring_send(h, 0, 0, 1, 1)
        ring_send(h, 0, 0, 2, 1)
        convert(spot(h, 0, 0))
        todo.append((h, 0, 0))

    def arrived(h, first, second):
        if second == 0:
            gathers[(h, 0, 0, first)].wait_recv()
            if first == 1:
                ring_send(h, 1, 0, 3, 0)
            ring_send(h, first, 0, 1, 1)
            ring_send(h, first, 0, 2, 1)
        else:
            gathers[(h, 1, first, second)].wait_recv()
            if second == 1:
                ring_send(h, first, 1, 3, 1)
        have(h, first, second)

    order = [(1, 0), (2, 0), (0, 1), (0, 2), (3, 0), (1, 1), (0, 3), (2, 1), (1, 2), (1, 3), (2, 2), (3, 1), (2, 3), (3, 2), (3, 3)]
    for first, second in order:
        for h in range(2):
            arrived(h, first, second)
    drain(0)
    for copy in sends:
        copy.wait_send()


def store_kernel(lens_ref, y_ref, kv_ref, cache_ref, y_out_ref, cache_buf, k_out_ref, v_out_ref, y_sem, out_sem):
    k_buf, v_buf = cache_buf.at[0], cache_buf.at[1]
    batch, pos_local, hd = k_buf.shape
    first_pos = lax.axis_index("sq") * pos_local
    row = lax.broadcasted_iota(jnp.int32, (16, hd), 0)
    pairs = ((k_buf, k_out_ref), (v_buf, v_out_ref))

    def write(c):
        at = pl.ds(pl.multiple_of(c * SEQS, SEQS), SEQS)
        return [pltpu.make_async_copy(buf.at[at], out.at[at], out_sem.at[w, c]) for w, (buf, out) in enumerate(pairs)]

    def replace(c, _):
        for i in range(SEQS):
            b = c * SEQS + i
            pos = lens_ref[b] - first_pos
            base = pl.multiple_of(lax.div(jnp.clip(pos, 0, pos_local - 1), 16) * 16, 16)
            here = row + base == pos
            for which, (buf, _) in enumerate(pairs):
                old = buf[b, pl.ds(base, 16), :].astype(jnp.float32)
                new = kv_ref[which, pl.ds(b, 1), :]
                buf[b, pl.ds(base, 16), :] = jnp.where(here, new, old).astype(jnp.bfloat16)
        for copy in write(c):
            copy.start()
        return 0

    def drain(c, _):
        for copy in write(c):
            copy.wait()
        return 0

    y_copy = pltpu.make_async_copy(y_ref, y_out_ref, y_sem)
    y_copy.start()
    lax.fori_loop(0, batch // SEQS, replace, 0)
    lax.fori_loop(0, batch // SEQS, drain, 0)
    y_copy.wait()


def solution(mesh):
    nx, ny = mesh.shape["sq"] // 2, mesh.shape["tp"]

    def local_step(hidden, cache_lens, k_cache, v_cache, ln_gain, ln_bias, w_query, b_query, w_kv, b_kv, w_out, b_out):
        batch, pos_local, hd = k_cache.shape
        d_model, depth = w_query.shape
        heads = depth // hd
        rows, cols = batch // (2 * nx), d_model // ny
        width = depth + hd
        half = cols // 2
        f32, bf16, dma, vmem_buf = jnp.float32, jnp.bfloat16, pltpu.SemaphoreType.DMA, pltpu.VMEM
        smem, vmem, hbm = (pl.BlockSpec(memory_space=m) for m in (pltpu.SMEM, pltpu.VMEM, pl.ANY))
        out_hidden, key_val, caches = pl.pallas_call(
            functools.partial(decode_kernel, (nx, ny, heads, rows, cols, pos_local)),
            out_shape=[
                vmem_buf((batch, d_model), bf16),
                vmem_buf((2, batch, hd), f32),
                vmem_buf((2,) + k_cache.shape, bf16),
            ],
            in_specs=[smem] + [vmem] * 5 + [hbm] * 6,
            out_specs=[vmem] * 3,
            scratch_shapes=[
                vmem_buf((W_SLOTS, d_model, WIDE), bf16),
                vmem_buf((batch * 16, hd), f32),
                vmem_buf((batch, width), f32),
                vmem_buf((SEQS * 16, hd), f32),
                vmem_buf((SEQS * 16, pos_local), f32),
                vmem_buf((SEQS * 16, pos_local), f32),
                vmem_buf((batch, hd), f32),
                vmem_buf((batch, hd), f32),
                vmem_buf((4, rows, width), f32),
                vmem_buf((3, rows, width), f32),
                vmem_buf((rows, depth), bf16),
                vmem_buf((4, 2, rows, half), f32),
                vmem_buf((3, 2, rows, half), f32),
                vmem_buf((rows, cols), bf16),
                vmem_buf((batch, d_model), f32),
                dma,
                dma((depth // WIDE + 1,)),
                dma((2, batch // SEQS)),
                dma((8, half // WIDE)),
                dma,
                dma((4,)),
                dma((4,)),
                dma((3,)),
                dma((3,)),
                dma((3, 2)),
                dma((3, 2)),
                dma((2, 15)),
                dma((2, 15)),
                dma((2, 16)),
                dma((2, 16)),
            ],
            compiler_params=pltpu.CompilerParams(collective_id=0, has_side_effects=True, vmem_limit_bytes=24 * 1024 * 1024),
            name="decode",
        )(
            cache_lens,
            ln_gain.reshape(1, d_model),
            ln_bias.reshape(1, d_model),
            b_query,
            b_kv.reshape(1, 2 * hd),
            b_out.reshape(1, d_model),
            hidden,
            w_query,
            w_kv,
            w_out,
            k_cache,
            v_cache,
        )
        out_hidden, _, key_new, val_new = pl.pallas_call(
            store_kernel,
            out_shape=[
                jax.ShapeDtypeStruct((batch, d_model), bf16),
                vmem_buf((2,) + k_cache.shape, bf16),
                jax.ShapeDtypeStruct(k_cache.shape, bf16),
                jax.ShapeDtypeStruct(v_cache.shape, bf16),
            ],
            in_specs=[smem] + [vmem] * 3,
            out_specs=[hbm, vmem, hbm, hbm],
            input_output_aliases={3: 1},
            scratch_shapes=[dma, dma((2, batch // SEQS))],
            compiler_params=pltpu.CompilerParams(vmem_limit_bytes=1 * 1024 * 1024),
            name="store",
        )(cache_lens, out_hidden, key_val, caches)
        return out_hidden, key_new, val_new

    cache_spec = P("dp", "sq", None)
    row_spec = P("dp", None)
    in_specs = (row_spec, P("dp"), cache_spec, cache_spec, P(None), P(None), P(None, "tp"), P("tp"), P(None, None), P(None), P("tp", None), P(None))
    out_specs = (row_spec, cache_spec, cache_spec)
    return jax.shard_map(local_step, mesh=mesh, in_specs=in_specs, out_specs=out_specs, check_vma=False)
```

time: 126 us -> 95.9 us (0.76)
  Pallas kernels: 54 us -> 94.9 us
  other arithmetic: 30.9 us -> 0 us
  matrix products: 30.1 us -> 0 us
  local copies, waits for them, and re-layouts: 9.79 us -> 0.01 us
    pallas_call x1 -> x2, Pallas kernels: 54 us -> 94.9 us  [the longest x1 82.2 us: local_step(): pl.pallas_call(functools.partial(decode_kernel, (nx, ny, heads, rows, col...]
    dot_general x4 -> x0, matrix products: 30.1 us -> none  [the longest x1 12.2 us: local_step(): jnp.einsum('bnd,btd->bnt', query, key_new, preferred_element_type=jnp.flo...]
    select_n x1 -> x0, other arithmetic: 23.3 us -> none  [local_step(): key_new = jnp.where(at_slot, key_val[:, None, :head_dim], k_cache)]
    reduce_sum x3 -> x0, other arithmetic: 7.43 us -> none  [the longest x1 3.9 us: local_step(): local_sum = jnp.sum(weights, axis=-1)]
    unnamed x23 -> x2, local copies, waits for them, and re-layouts: 3.54 us -> 0.01 us
    reshape x2 -> x0, local copies, waits for them, and re-layouts: 2.91 us -> none  [the longest x1 1.88 us: local_step(): numerator.reshape(batch, heads_local * head_dim)]
    dot_general x1 -> x0, local copies, waits for them, and re-layouts: 1.63 us -> none  [local_step(): jnp.einsum('bnt,btd->bnd', weights.astype(jnp.bfloat16), val_new, preferr...]
    concatenate x1 -> x0, local copies, waits for them, and re-layouts: 1.41 us -> none  [local_step(): jnp.concatenate([numerator.reshape(batch, heads_local * head_dim), jnp.pa...]
where the time goes in v5:
time: 95.9 us; the launch traced here: 95.7 us
  Pallas kernels  94.9 us (99%)
    pallas_call x1, Pallas kernels, local_step(): pl.pallas_call(functools.partial(decode_kernel, (nx, ny, heads, rows, col...  82.2 us
    pallas_call x1, Pallas kernels, local_step(): pl.pallas_call(store_kernel, out_shape=[jax.ShapeDtypeStruct((batch, d_mo...  12.7 us

profile of v5, /device:TPU:97, one launch (start us, length us, event | category | flops | bytes accessed | tf_op | source)
XLA Modules:
  0.0 95.7 jit_solution(17611621829857399806)
XLA Ops:
  0.6 0.0 copy-start
  0.6 82.2 %decode.1 = (bf16[256,6144]{1,0:T(8,128)(2,1)S(1)}, f32[2,256,128]{2,1,0:T(8,128)S(1)}, bf16[2,256,256,128]{3,2,1,0:T(8,128)(2,1)S(1)}) custom-call(s32[256]{0:T(256)} %lens_ref.3, f32[1,6144]{1,0:T(1,128)} %bitcast.4, f32[1,6144]{1,0:T(1,128)} %bitcast.5, f32[1536]{0:T(1024)} %b_query_ref.1, f32[1,256]{1,0:T(1,128)} %bitcast.7, f32[1,6144]{1,0:T(1,128)} %bitcast.6, ...), custom_call_target="tpu_custom_call" | custom-call | tf_op jit(solution)/shard_map/decode/pallas_call | solution.py:516
  82.9 0.0 copy-done
  82.9 12.7 %store.1 = (bf16[256,6144]{1,0:T(8,128)(2,1)}, bf16[2,256,256,128]{3,2,1,0:T(8,128)(2,1)S(1)}, bf16[256,256,128]{2,1,0:T(8,128)(2,1)}, bf16[256,256,128]{2,1,0:T(8,128)(2,1)}) custom-call(s32[256]{0:T(256)S(1)} %copy-done, bf16[256,6144]{1,0:T(8,128)(2,1)S(1)} %get-tuple-element.9.y_ref, ...), custom_call_target="tpu_custom_call", output_to_operand_aliasing={{1}: (3, {})} | custom-call | tf_op jit(solution)/shard_map/store/pallas_call | solution.py:573
Async XLA Ops:
  0.6 82.2 %copy-start = (s32[256]{0:T(256)S(1)}, s32[256]{0:T(256)}, u32[]{:S(2)}) copy-start(s32[256]{0:T(256)} %lens_ref.3) | copy-start | bytes 3076

commit v6 on v5

--- a/solution.py
+++ b/solution.py
@@ -10,7 +10,9 @@
 MESH = pl.DeviceIdType.MESH
 LANES = 128
 SEQS = 16
-WIDE = 256
+TALL = 1024
+WIDE = 512
+EARLY = 6
 W_SLOTS = 3
 
 
@@ -44,6 +46,7 @@
     kv_buf,
     cache_buf,
     w_buf,
+    wkv_buf,
     q_buf,
     part_buf,
     o_buf,
@@ -81,7 +84,7 @@
     half = cols // 2
     depth = heads * hd
     steps = batch // seqs
-    blocks = depth // WIDE
+    blocks = d_model // TALL
     sq = lax.axis_index("sq")
     y = lax.axis_index("tp")
     x = sq // 2
@@ -106,9 +109,12 @@
 
     h_buf = out_ref
 
-    def w_copy(k):
-        src = w_kv_ref if k == 0 else w_query_ref.at[:, (k - 1) * WIDE : k * WIDE]
-        return pltpu.make_async_copy(src, w_buf.at[k % W_SLOTS], w_sem.at[k])
+    def w_copies(k):
+        slot, at = k % W_SLOTS, pl.ds(k * TALL, TALL)
+        return (
+            pltpu.make_async_copy(w_query_ref.at[at, :], w_buf.at[pl.ds(slot * TALL, TALL), :], w_sem.at[0, k]),
+            pltpu.make_async_copy(w_kv_ref.at[at, :], wkv_buf.at[slot], w_sem.at[1, k]),
+        )
 
     def block_row(i):
         slot, mine = i // 2, i % 2
@@ -131,7 +137,11 @@
     h_copy = pltpu.make_async_copy(hidden_ref, h_buf, h_sem)
     h_copy.start()
     for k in range(W_SLOTS):
-        w_copy(k).start()
+        for copy in w_copies(k):
+            copy.start()
+    for c in range(EARLY):
+        for copy in read(c):
+            copy.start()
     q_buf[...] = jnp.zeros_like(q_buf)
     h_copy.wait()
 
@@ -175,51 +185,43 @@
     stat_buf2[...] = lax.rsqrt(row_means(stat_buf2) + 1e-5)
     lax.fori_loop(0, batch // 16, norm_rows, 0)
 
-    units = ((0, 0), (0, 1), (1, 0), (2, 0), (3, 0), (1, 1), (2, 1), (3, 1))
     y_order = (y_opp, y_bwd, y_fwd, y)
-    per_unit, per_slot = half // WIDE, d_model // depth
-
-    def wo_place(u, j):
-        at = (u % 4) * per_unit + j
-        return at // per_slot, slice((at % per_slot) * depth, (at % per_slot + 1) * depth)
-
-    def wo_copies(u):
-        target, h = units[u]
-        copies = []
-        for j in range(per_unit):
-            col = pl.multiple_of(y_order[target] * cols + h * half + j * WIDE, WIDE)
-            slot, at = wo_place(u, j)
-            copies.append(
-                pltpu.make_async_copy(w_out_ref.at[:, pl.ds(col, WIDE)], w_buf.at[slot, at, :], wo_sem.at[u, j])
-            )
-        return copies
-
-    for k in range(blocks + 1):
-        w_copy(k).wait()
-        acc = jnp.dot(h_buf[...], w_buf[k % W_SLOTS], preferred_element_type=jnp.float32)
-        if k == 0:
-            acc = (acc + b_kv_ref[...]).astype(jnp.bfloat16).astype(jnp.float32)
-            kv_buf[0] = acc[:, :hd]
-            kv_buf[1] = acc[:, hd:]
-        else:
-            bias = b_query_ref[(k - 1) * WIDE : k * WIDE].reshape(1, WIDE)
-            acc = (acc + bias).astype(jnp.bfloat16).astype(jnp.float32)
-            for e in range(WIDE // hd):
-                n = (k - 1) * (WIDE // hd) + e
-                q_buf[pl.ds(n, batch, stride=16), :] = acc[:, e * hd : (e + 1) * hd]
-        if k + W_SLOTS <= blocks:
-            w_copy(k + W_SLOTS).start()
-        if k + W_SLOTS == blocks:
-            for c in range(steps):
+
+    def wo_copy(k):
+        src = w_out_ref.at[:, pl.ds(pl.multiple_of(y_order[k] * cols, cols), cols)]
+        return pltpu.make_async_copy(src, w_buf.at[pl.ds((k % 2) * depth, depth), :], wo_sem.at[k])
+
+    for k in range(blocks):
+        for copy in w_copies(k):
+            copy.wait()
+        h_cols, slot = h_buf[:, k * TALL : (k + 1) * TALL], k % W_SLOTS
+        kv = jnp.dot(h_cols, wkv_buf[slot], preferred_element_type=jnp.float32)
+        for e in range(2):
+            part = kv[:, e * hd : (e + 1) * hd]
+            kv_buf[e] = part if k == 0 else kv_buf[e] + part
+        for n in range(0, depth, WIDE):
+            w_block = w_buf[slot * TALL : (slot + 1) * TALL, n : n + WIDE]
+            part = jnp.dot(h_cols, w_block, preferred_element_type=jnp.float32)
+            part_buf[:, n : n + WIDE] = part if k == 0 else part_buf[:, n : n + WIDE] + part
+        if k + W_SLOTS < blocks:
+            for copy in w_copies(k + W_SLOTS):
+                copy.start()
+        if k + W_SLOTS == blocks - 1:
+            for c in range(EARLY, steps):
                 for copy in read(c):
                     copy.start()
+    for e in range(2):
+        new = kv_buf[e] + b_kv_ref[:, e * hd : (e + 1) * hd]
+        kv_buf[e] = new.astype(jnp.bfloat16).astype(jnp.float32)
+    for n in range(heads):
+        new = part_buf[:, n * hd : (n + 1) * hd] + b_query_ref[n * hd : (n + 1) * hd].reshape(1, hd)
+        q_buf[pl.ds(n, batch, stride=16), :] = new.astype(jnp.bfloat16).astype(jnp.float32)
     hid_copy = pltpu.make_async_copy(
         hidden_ref.at[pl.ds(pl.multiple_of(sq * rows, rows), rows), pl.ds(pl.multiple_of(y * cols, cols), cols)], hid_buf, hid_sem
     )
     hid_copy.start()
-    for u in range(4):
-        for copy in wo_copies(u):
-            copy.start()
+    for k in range(2):
+        wo_copy(k).start()
 
     zero = jnp.zeros((16, hd), jnp.bfloat16)
     at_pos = lax.broadcasted_iota(jnp.int32, (16, pos_local), 1) + first_pos
@@ -340,40 +342,30 @@
         block = slice(n * hd, (n + 1) * hd)
         att_buf[:, block] = (total[:, block] / stat[:, 64 + n : 65 + n]).astype(jnp.bfloat16)
 
-    def project(u):
-        for copy in wo_copies(u):
-            copy.wait()
-        parts = []
-        for j in range(per_unit):
-            slot, at = wo_place(u, j)
-            parts.append(jnp.dot(att_buf[...], w_buf[slot, at, :], preferred_element_type=jnp.float32))
-        return jnp.concatenate(parts, axis=1)
-
-    def refill(u):
-        if u + 4 < len(units):
-            for copy in wo_copies(u + 4):
-                copy.start()
+    def project(k, h):
+        w_block = w_buf[(k % 2) * depth : (k % 2 + 1) * depth, h * half : (h + 1) * half]
+        return jnp.dot(att_buf[...], w_block, preferred_element_type=jnp.float32)
 
     y_o, y_b, y_a = [None, None], [None, None], [None, None]
-    for u, (target, h) in enumerate(units):
-        if target < 2:
-            proj_buf[target, h] = project(u)
-            refill(u)
-            peer = (to_y_fwd, to_y_bwd)[target]
-            copy = send(proj_buf.at[target, h], y_buf.at[target, h], y_send.at[target, h], y_recv.at[target, h], peer)
-            (y_o, y_b)[target][h] = copy
-        elif target == 2:
-            fwd_part = project(u)
-            refill(u)
-            y_o[h].wait_recv()
-            proj_buf[2, h] = fwd_part + y_buf[0, h]
-            y_a[h] = send(proj_buf.at[2, h], y_buf.at[2, h], y_send.at[2, h], y_recv.at[2, h], to_y_fwd)
-        else:
-            if h == 0:
-                hid_copy.wait()
-            own_cols = pl.ds(pl.multiple_of(y * cols + h * half, half), half)
-            proj_buf[3, h] = project(u) + hid_buf[:, h * half : (h + 1) * half].astype(jnp.float32) + b_out_ref[:, own_cols]
-            refill(u)
+    for k in range(4):
+        wo_copy(k).wait()
+        for h in range(2):
+            part = project(k, h)
+            if k < 2:
+                proj_buf[k, h] = part
+                copy = send(proj_buf.at[k, h], y_buf.at[k, h], y_send.at[k, h], y_recv.at[k, h], (to_y_fwd, to_y_bwd)[k])
+                (y_o, y_b)[k][h] = copy
+            elif k == 2:
+                y_o[h].wait_recv()
+                proj_buf[2, h] = part + y_buf[0, h]
+                y_a[h] = send(proj_buf.at[2, h], y_buf.at[2, h], y_send.at[2, h], y_recv.at[2, h], to_y_fwd)
+            else:
+                if h == 0:
+                    hid_copy.wait()
+                own_cols = pl.ds(pl.multiple_of(y * cols + h * half, half), half)
+                proj_buf[3, h] = part + hid_buf[:, h * half : (h + 1) * half].astype(jnp.float32) + b_out_ref[:, own_cols]
+        if k < 2:
+            wo_copy(k + 2).start()
 
     def place(xt, yt, ct, h):
         row = pl.multiple_of((xt * 2 + ct) * rows, rows)
@@ -523,7 +515,8 @@
             in_specs=[smem] + [vmem] * 5 + [hbm] * 6,
             out_specs=[vmem] * 3,
             scratch_shapes=[
-                vmem_buf((W_SLOTS, d_model, WIDE), bf16),
+                vmem_buf((W_SLOTS * TALL, depth), bf16),
+                vmem_buf((W_SLOTS, TALL, 2 * hd), bf16),
                 vmem_buf((batch * 16, hd), f32),
                 vmem_buf((batch, width), f32),
                 vmem_buf((SEQS * 16, hd), f32),
@@ -539,9 +532,9 @@
                 vmem_buf((rows, cols), bf16),
                 vmem_buf((batch, d_model), f32),
                 dma,
-                dma((depth // WIDE + 1,)),
+                dma((2, d_model // TALL)),
                 dma((2, batch // SEQS)),
-                dma((8, half // WIDE)),
+                dma((4,)),
                 dma,
                 dma((4,)),
                 dma((4,)),
@@ -554,7 +547,7 @@
                 dma((2, 16)),
                 dma((2, 16)),
             ],
-            compiler_params=pltpu.CompilerParams(collective_id=0, has_side_effects=True, vmem_limit_bytes=24 * 1024 * 1024),
+            compiler_params=pltpu.CompilerParams(collective_id=0, has_side_effects=True, vmem_limit_bytes=27 * 1024 * 1024),
             name="decode",
         )(
             cache_lens,

time: 95.9 us -> 93 us (0.970)
  Pallas kernels: 94.9 us -> 92 us
    pallas_call x1, Pallas kernels: 82.2 us -> 79.3 us  [local_step(): pl.pallas_call(functools.partial(decode_kernel, (nx, ny, heads, rows, col...]
where the time goes in v6:
time: 93 us; the launch traced here: 92.8 us
  Pallas kernels  92 us (99%)
    pallas_call x1, Pallas kernels, local_step(): pl.pallas_call(functools.partial(decode_kernel, (nx, ny, heads, rows, col...  79.3 us
    pallas_call x1, Pallas kernels, local_step(): pl.pallas_call(store_kernel, out_shape=[jax.ShapeDtypeStruct((batch, d_mo...  12.7 us

profile of v6, /device:TPU:97, one launch (start us, length us, event | category | flops | bytes accessed | tf_op | source)
XLA Modules:
  0.0 92.8 jit_solution(6374229958763862196)
XLA Ops:
  0.6 0.0 copy-start
  0.6 79.3 %decode.1 = (bf16[256,6144]{1,0:T(8,128)(2,1)S(1)}, f32[2,256,128]{2,1,0:T(8,128)S(1)}, bf16[2,256,256,128]{3,2,1,0:T(8,128)(2,1)S(1)}) custom-call(s32[256]{0:T(256)} %lens_ref.3, f32[1,6144]{1,0:T(1,128)} %bitcast.4, f32[1,6144]{1,0:T(1,128)} %bitcast.5, f32[1536]{0:T(1024)} %b_query_ref.1, f32[1,256]{1,0:T(1,128)} %bitcast.7, f32[1,6144]{1,0:T(1,128)} %bitcast.6, ...), custom_call_target="tpu_custom_call" | custom-call | tf_op jit(solution)/shard_map/decode/pallas_call | solution.py:508
  80.0 0.0 copy-done
  80.0 12.7 %store.1 = (bf16[256,6144]{1,0:T(8,128)(2,1)}, bf16[2,256,256,128]{3,2,1,0:T(8,128)(2,1)S(1)}, bf16[256,256,128]{2,1,0:T(8,128)(2,1)}, bf16[256,256,128]{2,1,0:T(8,128)(2,1)}) custom-call(s32[256]{0:T(256)S(1)} %copy-done, bf16[256,6144]{1,0:T(8,128)(2,1)S(1)} %get-tuple-element.9.y_ref, ...), custom_call_target="tpu_custom_call", output_to_operand_aliasing={{1}: (3, {})} | custom-call | tf_op jit(solution)/shard_map/store/pallas_call | solution.py:566
Async XLA Ops:
  0.6 79.3 %copy-start = (s32[256]{0:T(256)S(1)}, s32[256]{0:T(256)}, u32[]{:S(2)}) copy-start(s32[256]{0:T(256)} %lens_ref.3) | copy-start | bytes 3076

commit v7 on v6

--- a/solution.py
+++ b/solution.py
@@ -136,12 +136,19 @@
 
     h_copy = pltpu.make_async_copy(hidden_ref, h_buf, h_sem)
     h_copy.start()
-    for k in range(W_SLOTS):
+
+    def start_weights(k, _):
         for copy in w_copies(k):
             copy.start()
-    for c in range(EARLY):
+        return 0
+
+    def start_caches(c, _):
         for copy in read(c):
             copy.start()
+        return 0
+
+    lax.fori_loop(0, W_SLOTS, start_weights, 0)
+    lax.fori_loop(0, EARLY, start_caches, 0)
     q_buf[...] = jnp.zeros_like(q_buf)
     h_copy.wait()
 
@@ -207,9 +214,7 @@
             for copy in w_copies(k + W_SLOTS):
                 copy.start()
         if k + W_SLOTS == blocks - 1:
-            for c in range(EARLY, steps):
-                for copy in read(c):
-                    copy.start()
+            lax.fori_loop(EARLY, steps, start_caches, 0)
     for e in range(2):
         new = kv_buf[e] + b_kv_ref[:, e * hd : (e + 1) * hd]
         kv_buf[e] = new.astype(jnp.bfloat16).astype(jnp.float32)

time: 93 us -> 82.4 us (0.89)
  Pallas kernels: 92 us -> 81.4 us
    pallas_call x1, Pallas kernels: 79.3 us -> 68.8 us  [local_step(): pl.pallas_call(functools.partial(decode_kernel, (nx, ny, heads, rows, col...]
where the time goes in v7:
time: 82.4 us; the launch traced here: 82.2 us
  Pallas kernels  81.4 us (99%)
    pallas_call x1, Pallas kernels, local_step(): pl.pallas_call(functools.partial(decode_kernel, (nx, ny, heads, rows, col...  68.8 us
    pallas_call x1, Pallas kernels, local_step(): pl.pallas_call(store_kernel, out_shape=[jax.ShapeDtypeStruct((batch, d_mo...  12.7 us

profile of v7, /device:TPU:97, one launch (start us, length us, event | category | flops | bytes accessed | tf_op | source)
XLA Modules:
  0.0 82.2 jit_solution(15306899398939367997)
XLA Ops:
  0.6 0.0 copy-start
  0.6 68.8 %decode.1 = (bf16[256,6144]{1,0:T(8,128)(2,1)S(1)}, f32[2,256,128]{2,1,0:T(8,128)S(1)}, bf16[2,256,256,128]{3,2,1,0:T(8,128)(2,1)S(1)}) custom-call(s32[256]{0:T(256)} %lens_ref.3, f32[1,6144]{1,0:T(1,128)} %bitcast.4, f32[1,6144]{1,0:T(1,128)} %bitcast.5, f32[1536]{0:T(1024)} %b_query_ref.1, f32[1,256]{1,0:T(1,128)} %bitcast.7, f32[1,6144]{1,0:T(1,128)} %bitcast.6, ...), custom_call_target="tpu_custom_call" | custom-call | tf_op jit(solution)/shard_map/decode/pallas_call | solution.py:513
  69.4 0.0 copy-done
  69.4 12.7 %store.1 = (bf16[256,6144]{1,0:T(8,128)(2,1)}, bf16[2,256,256,128]{3,2,1,0:T(8,128)(2,1)S(1)}, bf16[256,256,128]{2,1,0:T(8,128)(2,1)}, bf16[256,256,128]{2,1,0:T(8,128)(2,1)}) custom-call(s32[256]{0:T(256)S(1)} %copy-done, bf16[256,6144]{1,0:T(8,128)(2,1)S(1)} %get-tuple-element.9.y_ref, ...), custom_call_target="tpu_custom_call", output_to_operand_aliasing={{1}: (3, {})} | custom-call | tf_op jit(solution)/shard_map/store/pallas_call | solution.py:571
Async XLA Ops:
  0.6 68.8 %copy-start = (s32[256]{0:T(256)S(1)}, s32[256]{0:T(256)}, u32[]{:S(2)}) copy-start(s32[256]{0:T(256)} %lens_ref.3) | copy-start | bytes 3076

commit v8 on v7

--- a/solution.py
+++ b/solution.py
@@ -134,8 +134,14 @@
             pltpu.make_async_copy(v_ref.at[at], v_buf.at[at], in_sem.at[1, c]),
         )
 
-    h_copy = pltpu.make_async_copy(hidden_ref, h_buf, h_sem)
-    h_copy.start()
+    h_parts = 4
+    h_rows = batch // h_parts
+    h_copies = [
+        pltpu.make_async_copy(hidden_ref.at[pl.ds(j * h_rows, h_rows), :], h_buf.at[pl.ds(j * h_rows, h_rows), :], h_sem.at[j])
+        for j in range(h_parts)
+    ]
+    for copy in h_copies:
+        copy.start()
 
     def start_weights(k, _):
         for copy in w_copies(k):
@@ -150,7 +156,6 @@
     lax.fori_loop(0, W_SLOTS, start_weights, 0)
     lax.fori_loop(0, EARLY, start_caches, 0)
     q_buf[...] = jnp.zeros_like(q_buf)
-    h_copy.wait()
 
     tiles = d_model // hd
 
@@ -186,11 +191,13 @@
     def row_means(buf):
         return jnp.broadcast_to(jnp.sum(buf[...], axis=-1, keepdims=True) * (1.0 / d_model), buf.shape)
 
-    lax.fori_loop(0, batch // 16, sum_rows, 0)
+    for j, copy in enumerate(h_copies):
+        copy.wait()
+        lax.fori_loop(j * h_rows // 16, (j + 1) * h_rows // 16, sum_rows, 0, unroll=2)
     stat_buf[...] = row_means(stat_buf)
-    lax.fori_loop(0, batch // 16, spread_rows, 0)
+    lax.fori_loop(0, batch // 16, spread_rows, 0, unroll=2)
     stat_buf2[...] = lax.rsqrt(row_means(stat_buf2) + 1e-5)
-    lax.fori_loop(0, batch // 16, norm_rows, 0)
+    lax.fori_loop(0, batch // 16, norm_rows, 0, unroll=2)
 
     y_order = (y_opp, y_bwd, y_fwd, y)
 
@@ -361,9 +368,7 @@
                 copy = send(proj_buf.at[k, h], y_buf.at[k, h], y_send.at[k, h], y_recv.at[k, h], (to_y_fwd, to_y_bwd)[k])
                 (y_o, y_b)[k][h] = copy
             elif k == 2:
-                y_o[h].wait_recv()
-                proj_buf[2, h] = part + y_buf[0, h]
-                y_a[h] = send(proj_buf.at[2, h], y_buf.at[2, h], y_send.at[2, h], y_recv.at[2, h], to_y_fwd)
+                proj_buf[2, h] = part
             else:
                 if h == 0:
                     hid_copy.wait()
@@ -371,6 +376,11 @@
                 proj_buf[3, h] = part + hid_buf[:, h * half : (h + 1) * half].astype(jnp.float32) + b_out_ref[:, own_cols]
         if k < 2:
             wo_copy(k + 2).start()
+        if k == 2:
+            for h in range(2):
+                y_o[h].wait_recv()
+                proj_buf[2, h] = proj_buf[2, h] + y_buf[0, h]
+                y_a[h] = send(proj_buf.at[2, h], y_buf.at[2, h], y_send.at[2, h], y_recv.at[2, h], to_y_fwd)
 
     def place(xt, yt, ct, h):
         row = pl.multiple_of((xt * 2 + ct) * rows, rows)
@@ -423,7 +433,7 @@
         pair_forward(h, first, second)
         convert(spot(h, first, second))
         todo.append((h, first, second))
-        drain(2)
+        drain(4)
 
     for h in range(2):
         y_b[h].wait_recv()
@@ -536,7 +546,7 @@
                 vmem_buf((3, 2, rows, half), f32),
                 vmem_buf((rows, cols), bf16),
                 vmem_buf((batch, d_model), f32),
-                dma,
+                dma((4,)),
                 dma((2, d_model // TALL)),
                 dma((2, batch // SEQS)),
                 dma((4,)),

time: 82.4 us -> 81.7 us (level)
  no operation moved by 1% of the time
where the time goes in v8:
time: 81.7 us; the launch traced here: 81.5 us
  Pallas kernels  80.7 us (99%)
  between operations  0.82 us (1%)
    pallas_call x1, Pallas kernels, local_step(): pl.pallas_call(functools.partial(decode_kernel, (nx, ny, heads, rows, col...  68 us
    pallas_call x1, Pallas kernels, local_step(): pl.pallas_call(store_kernel, out_shape=[jax.ShapeDtypeStruct((batch, d_mo...  12.7 us

profile of v8, /device:TPU:97, one launch (start us, length us, event | category | flops | bytes accessed | tf_op | source)
XLA Modules:
  0.0 81.5 jit_solution(2607166989515750673)
XLA Ops:
  0.6 0.0 copy-start
  0.6 68.0 %decode.1 = (bf16[256,6144]{1,0:T(8,128)(2,1)S(1)}, f32[2,256,128]{2,1,0:T(8,128)S(1)}, bf16[2,256,256,128]{3,2,1,0:T(8,128)(2,1)S(1)}) custom-call(s32[256]{0:T(256)} %lens_ref.3, f32[1,6144]{1,0:T(1,128)} %bitcast.4, f32[1,6144]{1,0:T(1,128)} %bitcast.5, f32[1536]{0:T(1024)} %b_query_ref.1, f32[1,256]{1,0:T(1,128)} %bitcast.7, f32[1,6144]{1,0:T(1,128)} %bitcast.6, ...), custom_call_target="tpu_custom_call" | custom-call | tf_op jit(solution)/shard_map/decode/pallas_call | solution.py:523
  68.7 0.0 copy-done
  68.7 12.7 %store.1 = (bf16[256,6144]{1,0:T(8,128)(2,1)}, bf16[2,256,256,128]{3,2,1,0:T(8,128)(2,1)S(1)}, bf16[256,256,128]{2,1,0:T(8,128)(2,1)}, bf16[256,256,128]{2,1,0:T(8,128)(2,1)}) custom-call(s32[256]{0:T(256)S(1)} %copy-done, bf16[256,6144]{1,0:T(8,128)(2,1)S(1)} %get-tuple-element.9.y_ref, ...), custom_call_target="tpu_custom_call", output_to_operand_aliasing={{1}: (3, {})} | custom-call | tf_op jit(solution)/shard_map/store/pallas_call | solution.py:581
Async XLA Ops:
  0.6 68.0 %copy-start = (s32[256]{0:T(256)S(1)}, s32[256]{0:T(256)}, u32[]{:S(2)}) copy-start(s32[256]{0:T(256)} %lens_ref.3) | copy-start | bytes 3076

commit v9 on v8

--- a/solution.py
+++ b/solution.py
@@ -9,10 +9,11 @@
 
 MESH = pl.DeviceIdType.MESH
 LANES = 128
-SEQS = 16
+SEQS = 32
 TALL = 1024
 WIDE = 512
-EARLY = 6
+STORE_SEQS = 16
+EARLY = 3
 W_SLOTS = 3
 
 
@@ -319,19 +320,22 @@
     pl.semaphore_wait(barrier, 5)
     score(0, s_buf0)
 
-    def one_block(i, _):
-        c = i * 2
+    def two_blocks(t, _):
+        c = t * 2
         score(c + 1, s_buf1)
         combine(c, s_buf0)
+        for j in range(3):
+            pl.when(t == j)(functools.partial(after_block, 2 * j))
         score(c + 2, s_buf0)
         combine(c + 1, s_buf1)
-        for j in range(7):
-            pl.when(i == j)(functools.partial(after_block, j))
-        return 0
-
-    lax.fori_loop(0, steps // 2 - 1, one_block, 0)
+        for j in range(3):
+            pl.when(t == j)(functools.partial(after_block, 2 * j + 1))
+        return 0
+
+    lax.fori_loop(0, steps // 2 - 1, two_blocks, 0)
     score(steps - 1, s_buf1)
     combine(steps - 2, s_buf0)
+    after_block(6)
     combine(steps - 1, s_buf1)
 
     own = pl.multiple_of(sq * rows, rows)
@@ -479,12 +483,12 @@
     pairs = ((k_buf, k_out_ref), (v_buf, v_out_ref))
 
     def write(c):
-        at = pl.ds(pl.multiple_of(c * SEQS, SEQS), SEQS)
+        at = pl.ds(pl.multiple_of(c * STORE_SEQS, STORE_SEQS), STORE_SEQS)
         return [pltpu.make_async_copy(buf.at[at], out.at[at], out_sem.at[w, c]) for w, (buf, out) in enumerate(pairs)]
 
     def replace(c, _):
-        for i in range(SEQS):
-            b = c * SEQS + i
+        for i in range(STORE_SEQS):
+            b = c * STORE_SEQS + i
             pos = lens_ref[b] - first_pos
             base = pl.multiple_of(lax.div(jnp.clip(pos, 0, pos_local - 1), 16) * 16, 16)
             here = row + base == pos
@@ -503,8 +507,8 @@
 
     y_copy = pltpu.make_async_copy(y_ref, y_out_ref, y_sem)
     y_copy.start()
-    lax.fori_loop(0, batch // SEQS, replace, 0)
-    lax.fori_loop(0, batch // SEQS, drain, 0)
+    lax.fori_loop(0, batch // STORE_SEQS, replace, 0)
+    lax.fori_loop(0, batch // STORE_SEQS, drain, 0)
     y_copy.wait()
 
 
@@ -562,7 +566,7 @@
                 dma((2, 16)),
                 dma((2, 16)),
             ],
-            compiler_params=pltpu.CompilerParams(collective_id=0, has_side_effects=True, vmem_limit_bytes=27 * 1024 * 1024),
+            compiler_params=pltpu.CompilerParams(collective_id=0, has_side_effects=True, vmem_limit_bytes=28 * 1024 * 1024),
             name="decode",
         )(
             cache_lens,
@@ -589,7 +593,7 @@
             in_specs=[smem] + [vmem] * 3,
             out_specs=[hbm, vmem, hbm, hbm],
             input_output_aliases={3: 1},
-            scratch_shapes=[dma, dma((2, batch // SEQS))],
+            scratch_shapes=[dma, dma((2, batch // STORE_SEQS))],
             compiler_params=pltpu.CompilerParams(vmem_limit_bytes=1 * 1024 * 1024),
             name="store",
         )(cache_lens, out_hidden, key_val, caches)

time: 81.7 us -> 81.5 us (level)
  no operation moved by 1% of the time
where the time goes in v9:
time: 81.5 us; the launch traced here: 81.3 us
  Pallas kernels  80.5 us (99%)
  between operations  0.82 us (1%)
    pallas_call x1, Pallas kernels, local_step(): pl.pallas_call(functools.partial(decode_kernel, (nx, ny, heads, rows, col...  67.8 us
    pallas_call x1, Pallas kernels, local_step(): pl.pallas_call(store_kernel, out_shape=[jax.ShapeDtypeStruct((batch, d_mo...  12.7 us

profile of v9, /device:TPU:97, one launch (start us, length us, event | category | flops | bytes accessed | tf_op | source)
XLA Modules:
  0.0 81.3 jit_solution(17339188634589544036)
XLA Ops:
  0.6 0.0 copy-start
  0.6 67.8 %decode.1 = (bf16[256,6144]{1,0:T(8,128)(2,1)S(1)}, f32[2,256,128]{2,1,0:T(8,128)S(1)}, bf16[2,256,256,128]{3,2,1,0:T(8,128)(2,1)S(1)}) custom-call(s32[256]{0:T(256)} %lens_ref.3, f32[1,6144]{1,0:T(1,128)} %bitcast.4, f32[1,6144]{1,0:T(1,128)} %bitcast.5, f32[1536]{0:T(1024)} %b_query_ref.1, f32[1,256]{1,0:T(1,128)} %bitcast.7, f32[1,6144]{1,0:T(1,128)} %bitcast.6, ...), custom_call_target="tpu_custom_call" | custom-call | tf_op jit(solution)/shard_map/decode/pallas_call | solution.py:527
  68.5 0.0 copy-done
  68.5 12.7 %store.1 = (bf16[256,6144]{1,0:T(8,128)(2,1)}, bf16[2,256,256,128]{3,2,1,0:T(8,128)(2,1)S(1)}, bf16[256,256,128]{2,1,0:T(8,128)(2,1)}, bf16[256,256,128]{2,1,0:T(8,128)(2,1)}) custom-call(s32[256]{0:T(256)S(1)} %copy-done, bf16[256,6144]{1,0:T(8,128)(2,1)S(1)} %get-tuple-element.9.y_ref, ...), custom_call_target="tpu_custom_call", output_to_operand_aliasing={{1}: (3, {})} | custom-call | tf_op jit(solution)/shard_map/store/pallas_call | solution.py:585
Async XLA Ops:
  0.6 67.8 %copy-start = (s32[256]{0:T(256)S(1)}, s32[256]{0:T(256)}, u32[]{:S(2)}) copy-start(s32[256]{0:T(256)} %lens_ref.3) | copy-start | bytes 3076

commit v10 on v9

--- a/solution.py
+++ b/solution.py
@@ -10,11 +10,11 @@
 MESH = pl.DeviceIdType.MESH
 LANES = 128
 SEQS = 32
-TALL = 1024
+TALL = 768
 WIDE = 512
 STORE_SEQS = 16
 EARLY = 3
-W_SLOTS = 3
+W_SLOTS = 4
 
 
 def merge_into(dst, part_a, part_b, heads):
@@ -466,7 +466,7 @@
                 ring_send(h, first, 1, 3, 1)
         have(h, first, second)
 
-    order = [(1, 0), (2, 0), (0, 1), (0, 2), (3, 0), (1, 1), (0, 3), (2, 1), (1, 2), (1, 3), (2, 2), (3, 1), (2, 3), (3, 2), (3, 3)]
+    order = [(1, 0), (2, 0), (0, 1), (0, 2), (1, 1), (3, 0), (1, 2), (2, 1), (0, 3), (2, 2), (3, 1), (1, 3), (3, 2), (2, 3), (3, 3)]
     for first, second in order:
         for h in range(2):
             arrived(h, first, second)

time: 81.5 us -> 81.2 us (level)
  no operation moved by 1% of the time
where the time goes in v10:
time: 81.2 us; the launch traced here: 81 us
  Pallas kernels  80.2 us (99%)
  between operations  0.82 us (1%)
    pallas_call x1, Pallas kernels, local_step(): pl.pallas_call(functools.partial(decode_kernel, (nx, ny, heads, rows, col...  67.5 us
    pallas_call x1, Pallas kernels, local_step(): pl.pallas_call(store_kernel, out_shape=[jax.ShapeDtypeStruct((batch, d_mo...  12.7 us

profile of v10, /device:TPU:97, one launch (start us, length us, event | category | flops | bytes accessed | tf_op | source)
XLA Modules:
  0.0 81.0 jit_solution(13810231501275688718)
XLA Ops:
  0.6 0.0 copy-start
  0.6 67.5 %decode.1 = (bf16[256,6144]{1,0:T(8,128)(2,1)S(1)}, f32[2,256,128]{2,1,0:T(8,128)S(1)}, bf16[2,256,256,128]{3,2,1,0:T(8,128)(2,1)S(1)}) custom-call(s32[256]{0:T(256)} %lens_ref.3, f32[1,6144]{1,0:T(1,128)} %bitcast.4, f32[1,6144]{1,0:T(1,128)} %bitcast.5, f32[1536]{0:T(1024)} %b_query_ref.1, f32[1,256]{1,0:T(1,128)} %bitcast.7, f32[1,6144]{1,0:T(1,128)} %bitcast.6, ...), custom_call_target="tpu_custom_call" | custom-call | tf_op jit(solution)/shard_map/decode/pallas_call | solution.py:527
  68.2 0.0 copy-done
  68.2 12.7 %store.1 = (bf16[256,6144]{1,0:T(8,128)(2,1)}, bf16[2,256,256,128]{3,2,1,0:T(8,128)(2,1)S(1)}, bf16[256,256,128]{2,1,0:T(8,128)(2,1)}, bf16[256,256,128]{2,1,0:T(8,128)(2,1)}) custom-call(s32[256]{0:T(256)S(1)} %copy-done, bf16[256,6144]{1,0:T(8,128)(2,1)S(1)} %get-tuple-element.9.y_ref, ...), custom_call_target="tpu_custom_call", output_to_operand_aliasing={{1}: (3, {})} | custom-call | tf_op jit(solution)/shard_map/store/pallas_call | solution.py:585
Async XLA Ops:
  0.6 67.5 %copy-start = (s32[256]{0:T(256)S(1)}, s32[256]{0:T(256)}, u32[]{:S(2)}) copy-start(s32[256]{0:T(256)} %lens_ref.3) | copy-start | bytes 3076

commit v11 on v10

--- a/solution.py
+++ b/solution.py
@@ -437,7 +437,7 @@
         pair_forward(h, first, second)
         convert(spot(h, first, second))
         todo.append((h, first, second))
-        drain(4)
+        drain(6)
 
     for h in range(2):
         y_b[h].wait_recv()

time: 81.2 us -> 81.2 us (level)
  no operation moved by 1% of the time
where the time goes in v11:
time: 81.2 us; the launch traced here: 81 us
  Pallas kernels  80.2 us (99%)
  between operations  0.82 us (1%)
    pallas_call x1, Pallas kernels, local_step(): pl.pallas_call(functools.partial(decode_kernel, (nx, ny, heads, rows, col...  67.5 us
    pallas_call x1, Pallas kernels, local_step(): pl.pallas_call(store_kernel, out_shape=[jax.ShapeDtypeStruct((batch, d_mo...  12.7 us

profile of v11, /device:TPU:97, one launch (start us, length us, event | category | flops | bytes accessed | tf_op | source)
XLA Modules:
  0.0 81.0 jit_solution(17248737892251027590)
XLA Ops:
  0.6 0.0 copy-start
  0.6 67.5 %decode.1 = (bf16[256,6144]{1,0:T(8,128)(2,1)S(1)}, f32[2,256,128]{2,1,0:T(8,128)S(1)}, bf16[2,256,256,128]{3,2,1,0:T(8,128)(2,1)S(1)}) custom-call(s32[256]{0:T(256)} %lens_ref.3, f32[1,6144]{1,0:T(1,128)} %bitcast.4, f32[1,6144]{1,0:T(1,128)} %bitcast.5, f32[1536]{0:T(1024)} %b_query_ref.1, f32[1,256]{1,0:T(1,128)} %bitcast.7, f32[1,6144]{1,0:T(1,128)} %bitcast.6, ...), custom_call_target="tpu_custom_call" | custom-call | tf_op jit(solution)/shard_map/decode/pallas_call | solution.py:527
  68.2 0.0 copy-done
  68.2 12.7 %store.1 = (bf16[256,6144]{1,0:T(8,128)(2,1)}, bf16[2,256,256,128]{3,2,1,0:T(8,128)(2,1)S(1)}, bf16[256,256,128]{2,1,0:T(8,128)(2,1)}, bf16[256,256,128]{2,1,0:T(8,128)(2,1)}) custom-call(s32[256]{0:T(256)S(1)} %copy-done, bf16[256,6144]{1,0:T(8,128)(2,1)S(1)} %get-tuple-element.9.y_ref, ...), custom_call_target="tpu_custom_call", output_to_operand_aliasing={{1}: (3, {})} | custom-call | tf_op jit(solution)/shard_map/store/pallas_call | solution.py:585
Async XLA Ops:
  0.6 67.5 %copy-start = (s32[256]{0:T(256)S(1)}, s32[256]{0:T(256)}, u32[]{:S(2)}) copy-start(s32[256]{0:T(256)} %lens_ref.3) | copy-start | bytes 3076
